TPU v7x, 128 devices: a whole 4x4x4 slice. The times are simulated.
128 devices in a mesh: dp: 128 (over z, y, x, core).
Axes of the slice: x: 4, y: 4, z: 4, core: 2. Of those that a mesh axis runs over, the one named last changes fastest.
Arguments:
- attended: bfloat16 [65536, 1152], P('dp'), may hold values from -24 to 24, as said below
- proj_cot: bfloat16 [65536, 1152], P('dp'), may hold values from -0.00036621094 to 0.00036621094
- timesteps: float32 [256], P('dp'), may hold values from 0 to 1
- embed_cot: bfloat16 [256, 1152], P('dp'), may hold values from -0.015625 to 0.015625
- master_proj: float32 [1327104], P('dp'), may hold values from -0.1875 to 0.1875
- moment_proj: float32 [1327104], P('dp'), may hold values from -0.013671875 to 0.013671875
- second_proj: float32 [1327104], P('dp'), may hold values from 1.8838011e-07 to 3.0140818e-06
- master_embed: float32 [294912], P('dp'), may hold values from -0.375 to 0.375
- moment_embed: float32 [294912], P('dp'), may hold values from -0.02734375 to 0.02734375
- squared_moment_layer: float32 [294912], P('dp'), may hold values from 8.477105e-07 to 1.3563368e-05
- attended_next: bfloat16 [65536, 1152], P('dp'), may hold values from -6 to 6
- timesteps_next: float32 [256], P('dp'), may hold values from 0 to 1
Outputs:
- next_proj: bfloat16 [65536, 1152], P('dp')
- next_embed: bfloat16 [256, 1152], P('dp')
- move_direction_output: float32 [1327104], P('dp')
- step_embed: float32 [294912], P('dp')
- master_proj_new: float32 [1327104], P('dp')
- master_embed_new: float32 [294912], P('dp')
- grad_norm: float32 [], replicated
Inputs may be any that keep to these rules, and one draw needn't show every extreme that they name: attended has entries of mean zero whose scale differs between feature columns by up to a factor of 16.
All inputs are finite; a program needn't handle non-finite values.
Results may differ from a plain program's by a relative error of at most 0.0025.
Values may be sent and summed in bfloat16 or wider, within the bound.
A program may use at most 64 MiB of HBM per device.

v0:
```python
import math

import jax
import jax.numpy as jnp
from jax import lax
from jax.sharding import Mesh
from jax.sharding import PartitionSpec as P

DP = ("dp_0", "dp_1", "dp_2", "dp_3")


beta_one = 0.9
beta_two = 0.999
step_count = 1000.0
learn_rate = 0.0001
shrink_factor = 0.01
epsilon = 1e-08
max_norm = 1.0


def over_axes(value, axes):
    for axis in axes:
        value = lax.psum(value, axis)
    return value


def joined_along(blocks, dim):
    lengths = list(blocks.shape[1:])
    lengths[dim] *= blocks.shape[0]
    return jnp.moveaxis(blocks, 0, dim).reshape(lengths)


def gather_packed(arrays, axis, dims):
    flat = jnp.concatenate([a.reshape(-1) for a in arrays])
    lines, at, finished = lax.all_gather(flat, axis), 0, []
    for a, dim in zip(arrays, dims):
        blocks = lines[:, at : at + a.size].reshape(-1, *a.shape)
        finished.append(joined_along(blocks, dim))
        at += a.size
    return tuple(finished)


def freq_embed(moments, width):
    half_width = width // 2
    ladder = jnp.arange(half_width, dtype=jnp.float32)
    freqs = jnp.exp(-math.log(10000.0) * ladder / half_width)
    phase_values = (moments * 1000.0)[:, None] * freqs[None, :]
    return jnp.concatenate([jnp.cos(phase_values), jnp.sin(phase_values)], axis=1).astype(
        jnp.bfloat16
    )


def adamw_update(gradient, clip, master, moment, second):
    scaled = clip * gradient
    first_new = beta_one * moment + (1.0 - beta_one) * scaled
    second_new = beta_two * second + (1.0 - beta_two) * scaled * scaled
    first_hat = first_new / (1.0 - beta_one**step_count)
    second_hat = second_new / (1.0 - beta_two**step_count)
    direction = first_hat / (jnp.sqrt(second_hat) + epsilon)
    freshened_values = master - learn_rate * (direction + shrink_factor * master)
    return (direction, freshened_values)


def shards(
    attended,
    proj_cot,
    timesteps,
    embed_cot,
    master_proj,
    moment_proj,
    second_proj,
    master_embed,
    moment_embed,
    squared_moment_layer,
    attended_next,
    timesteps_next,
):
    width = attended.shape[1]
    freq_width = master_embed.shape[0] * lax.axis_size(DP) // width
    term_proj = jnp.dot(attended.T, proj_cot, preferred_element_type=jnp.float32).reshape(-1)
    freq_now = freq_embed(timesteps, freq_width)
    term_embed = jnp.dot(freq_now.T, embed_cot, preferred_element_type=jnp.float32).reshape(-1)
    grad_proj, grad_embed = (
        lax.psum_scatter(term_proj, DP, scatter_dimension=0, tiled=True),
        lax.psum_scatter(term_embed, DP, scatter_dimension=0, tiled=True),
    )
    square_proj = over_axes(jnp.sum(grad_proj * grad_proj), DP)
    square_embed = over_axes(jnp.sum(grad_embed * grad_embed), DP)
    total = square_proj + square_embed
    grad_norm = jnp.sqrt(total)
    clip = jnp.minimum(jnp.float32(1.0), max_norm / (grad_norm + 1e-06))
    move_direction_output, master_proj_new = adamw_update(
        grad_proj, clip, master_proj, moment_proj, second_proj
    )
    step_embed, master_embed_new = adamw_update(
        grad_embed, clip, master_embed, moment_embed, squared_moment_layer
    )
    shard_proj = master_proj_new.astype(jnp.bfloat16)
    shard_embed = master_embed_new.astype(jnp.bfloat16)
    whole_proj, whole_embed = gather_packed((shard_proj, shard_embed), DP, (0, 0))
    weight_proj = whole_proj.reshape(width, width)
    weight_embed = whole_embed.reshape(freq_width, width)
    next_proj = jnp.dot(attended_next, weight_proj, preferred_element_type=jnp.float32).astype(
        jnp.bfloat16
    )
    freq_next = freq_embed(timesteps_next, freq_width)
    next_embed = jnp.dot(freq_next, weight_embed, preferred_element_type=jnp.float32).astype(
        jnp.bfloat16
    )
    return (
        next_proj,
        next_embed,
        move_direction_output,
        step_embed,
        master_proj_new,
        master_embed_new,
        grad_norm,
    )


def solution(mesh):
    finer = Mesh(mesh.devices.reshape(4, 4, 4, 2), ("dp_0", "dp_1", "dp_2", "dp_3"))
    return jax.shard_map(
        shards,
        mesh=finer,
        in_specs=(
            P(DP, None),
            P(DP, None),
            P(DP),
            P(DP, None),
            P(DP),
            P(DP),
            P(DP),
            P(DP),
            P(DP),
            P(DP),
            P(DP, None),
            P(DP),
        ),
        out_specs=(P(DP, None), P(DP, None), P(DP), P(DP), P(DP), P(DP), P()),
        check_vma=False,
    )
```

profile of v0, /device:TPU:1, one launch (start us, length us, event | category | flops | bytes accessed | tf_op | source)
XLA Modules:
  0.0 315.7 jit_solution(12199632284855341670)
XLA Ops:
  7.2 0.0 copy-start
  7.2 0.0 all-reduce.5.cloned.1.call-start
  7.2 0.8 broadcast_multiply_fusion
  8.0 0.1 fusion.13
  8.1 1.1 fusion.15
  9.2 0.0 copy-start.1
  9.2 1.1 reshape.28
  10.3 0.0 copy-done
  10.3 0.6 copy-done.1
  10.9 4.1 %fusion.28 = f32[1152,1152]{1,0:T(8,128)} fusion(bf16[512,1152]{1,0:T(8,128)(2,1)S(1)} %copy-done, bf16[512,1152]{1,0:T(8,128)(2,1)S(1)} %copy-done.1), kind=kOutput, calls=%fused_computation.43 | convolution fusion | flops 1358954496 | bytes 7667712 | tf_op jit(solution)/shard_map/dot_general | solution.py:80
  15.0 6.6 %reshape.27 = f32[1327104]{0:T(1024)} reshape(f32[1152,1152]{1,0:T(8,128)} %fusion.28) | data formatting | bytes 10616832 | tf_op jit(solution)/shard_map/reshape | solution.py:80
  21.5 0.0 copy-start.2
  21.5 0.0 copy-start.3
  21.5 0.0 copy-start.4
  21.5 0.0 copy-start.5
  21.5 0.0 copy-start.6
  21.5 0.0 copy-start.7
  21.5 0.0 all-reduce.5.cloned.1.call-update
  21.6 0.0 all-gather.4.cloned.1.call-start
  21.6 162.6 %all-reduce.5.cloned.1.call-done = (f32[294912]{0:T(1024)}, f32[1327104]{0:T(1024)}) async-done(((f32[294912]{0:T(1024)}, f32[1327104]{0:T(1024)}), (f32[294912]{0:T(1024)}, f32[1327104]{0:T(1024)})) %all-reduce.5.cloned.1.call-update) | async-done | bytes 6488080
  184.2 1.5 multiply_reduce_fusion
  185.7 1.4 multiply_reduce_fusion.1
  188.4 8.8 %psum.67 = f32[]{:T(128)} all-reduce(f32[]{:T(128)S(6)} %add.56), channel_id=1, replica_groups=mesh['dp_0'=4,'dp_1'=4,'dp_2'=4,'dp_3'=2] {'dp_0'}, use_global_device_ids=true, to_apply=%region_2.0 | all-reduce | flops 1 | bytes 8 | tf_op jit(solution)/shard_map/psum | solution.py:23
  197.2 8.3 %psum.66 = f32[]{:T(128)} all-reduce(f32[]{:T(128)} %psum.67), channel_id=1, replica_groups=mesh['dp_0'=4,'dp_1'=4,'dp_2'=4,'dp_3'=2] {'dp_1'}, use_global_device_ids=true, to_apply=%region_3.0 | all-reduce | flops 1 | bytes 8 | tf_op jit(solution)/shard_map/psum | solution.py:23
  205.5 7.2 %psum.65 = f32[]{:T(128)} all-reduce(f32[]{:T(128)} %psum.66), channel_id=1, replica_groups=mesh['dp_0'=4,'dp_1'=4,'dp_2'=4,'dp_3'=2] {'dp_2'}, use_global_device_ids=true, to_apply=%region_4.0 | all-reduce | flops 1 | bytes 8 | tf_op jit(solution)/shard_map/psum | solution.py:23
  212.8 9.2 %psum.64 = f32[]{:T(128)} all-reduce(f32[]{:T(128)} %psum.65), channel_id=1, replica_groups=mesh['dp_0'=4,'dp_1'=4,'dp_2'=4,'dp_3'=2] {'dp_3'}, use_global_device_ids=true, to_apply=%region_5.0 | all-reduce | flops 1 | bytes 8 | tf_op jit(solution)/shard_map/psum | solution.py:23
  222.6 0.0 copy-done.2
  222.7 0.0 copy-done.3
  222.7 0.0 copy-done.4
  222.7 1.6 fusion.24
  224.2 0.0 copy-done.5
  224.2 0.0 copy-done.6
  224.2 0.0 copy-done.7
  224.2 1.4 fusion.26
  225.7 0.6 reshape.30
  226.3 0.0 all-gather.4.cloned.1.call-update
  226.4 63.9 %all-gather.4.cloned.1.call-done = bf16[128,1,12672]{2,1,0:T(2,128)(2,1)} async-done(((bf16[1,1,12672]{2,1,0:T(2,128)(2,1)}), bf16[128,1,12672]{2,1,0:T(2,128)(2,1)}) %all-gather.4.cloned.1.call-update) | async-done | bytes 3244048 | tf_op jit(solution)/shard_map/all_gather | solution.py:35
  290.3 3.2 %copy.24 = bf16[128,1,12672]{2,0,1:T(8,128)(2,1)S(1)} copy(bf16[128,1,12672]{2,1,0:T(2,128)(2,1)} %all-gather.4.cloned.1.call-done) | data formatting | bytes 6488064
  293.4 1.7 slice.8
  295.2 6.4 %reshape_reshape.6 = bf16[1152,1152]{1,0:T(8,128)(2,1)} reshape(bf16[128,10368]{1,0:T(8,128)(2,1)} %slice.8) | data formatting | bytes 5308416 | tf_op jit(solution)/shard_map/reshape;reshape | solution.py:101
  301.6 3.8 %fusion = bf16[512,1152]{0,1:T(8,128)(2,1)S(1)} fusion(bf16[1152,1152]{1,0:T(8,128)(2,1)} %reshape_reshape.6, bf16[512,1152]{1,0:T(8,128)(2,1)} %param.22), kind=kOutput, calls=%fused_computation.2 | convolution fusion | flops 1359544320 | bytes 5013504 | tf_op jit(solution)/shard_map/dot_general | solution.py:103
  305.4 1.4 copy.21
  306.8 0.2 reshape_reshape.7
  307.0 0.8 convolution_convert_fusion.1
  (3 shorter events, 0.1 us)
Async XLA Ops:
  7.2 3.1 copy-start
  7.2 177.0 %all-reduce.5.cloned.1.call-start = ((), (), s32[]{:S(2)}) async-start(), calls=%async_computation.1 | async-start | bytes 12976128
  9.2 1.7 copy-start.1
  21.5 201.1 %copy-start.2 = (f32[10368]{0:T(1024)S(1)}, f32[10368]{0:T(1024)}, u32[]{:S(2)}) copy-start(f32[10368]{0:T(1024)} %param.16) | copy-start | bytes 124420
  21.5 201.1 %copy-start.3 = (f32[10368]{0:T(1024)S(1)}, f32[10368]{0:T(1024)}, u32[]{:S(2)}) copy-start(f32[10368]{0:T(1024)} %param.18) | copy-start | bytes 124420
  21.5 201.2 %copy-start.4 = (f32[10368]{0:T(1024)S(1)}, f32[10368]{0:T(1024)}, u32[]{:S(2)}) copy-start(f32[10368]{0:T(1024)} %param.17) | copy-start | bytes 124420
  21.5 202.7 %copy-start.5 = (f32[2304]{0:T(1024)S(1)}, f32[2304]{0:T(1024)}, u32[]{:S(2)}) copy-start(f32[2304]{0:T(1024)} %param.19) | copy-start | bytes 27652
  21.5 202.7 %copy-start.6 = (f32[2304]{0:T(1024)S(1)}, f32[2304]{0:T(1024)}, u32[]{:S(2)}) copy-start(f32[2304]{0:T(1024)} %param.21) | copy-start | bytes 27652
  21.5 202.7 %copy-start.7 = (f32[2304]{0:T(1024)S(1)}, f32[2304]{0:T(1024)}, u32[]{:S(2)}) copy-start(f32[2304]{0:T(1024)} %param.20) | copy-start | bytes 27652
  21.6 268.7 %all-gather.4.cloned.1.call-start = ((), (), s32[]{:S(2)}) async-start(), calls=%async_computation | async-start | bytes 6538752 | tf_op jit(solution)/shard_map/all_gather | solution.py:35
Sparse Core Ops, SparseCore 0:
  21.7 162.4 all-reduce.4
  226.5 63.7 all-gather.3
where the time goes:
time: 317 us; the launch traced here: 316 us
  waiting for transfers between devices  227 us (72%)
  blocking collectives  33.5 us (11%)
  local copies, waits for them, and re-layouts  21.8 us (7%)
  between operations  17.3 us (5%)
  matrix products  9.74 us (3%)
  other arithmetic  6.77 us (2%)
    unnamed x3, waiting for transfers between devices  163 us
    all_gather x1, waiting for transfers between devices, gather_packed(): lines, at, finished = (lax.all_gather(flat, axis), 0, [])  63.9 us
    psum x4, blocking collectives, over_axes(): value = lax.psum(value, axis)  33.5 us
    reshape x1, local copies, waits for them, and re-layouts, shards(): jnp.dot(attended.T, proj_cot, preferred_element_type=jnp.float32)  6.55 us
    another operation x1, local copies, waits for them, and re-layouts, shards(): weight_proj = whole_proj.reshape(width, width)  6.36 us
  transfers between devices with their start and end apart: 2, of which 2 were waited for; matrix products, arithmetic and copies ran while one was open for 0% of the time, Pallas kernels for 0%

commit v1 on v0

v1 whole, which is shorter than its diff:
```python
import functools
import math

import jax
import jax.numpy as jnp
from jax import lax
from jax.experimental import pallas as pl
from jax.experimental.pallas import tpu as pltpu
from jax.sharding import Mesh
from jax.sharding import PartitionSpec as P

AXES = ("z", "y", "x", "c")
MESH = pl.DeviceIdType.MESH
F32 = jnp.float32
BF16 = jnp.bfloat16

beta_one = 0.9
beta_two = 0.999
step_count = 1000.0
learn_rate = 0.0001
shrink_factor = 0.01
epsilon = 1e-08
max_norm = 1.0

TILES = 9
MINE = {0: (0, 5), 1: (5, 4)}
UNITS = {
    0: ((0, 0, 2), (1, 2, 2), (2, 4, 1)),
    1: ((0, 0, 1), (1, 1, 1), (2, 2, 2)),
}
EUNIT = {0: (2, 0, 5), 1: (0, 0, 4)}
SLOTS = 5


def adamw_update(gradient, clip, master, moment, second):
    scaled = clip * gradient
    first_new = beta_one * moment + (1.0 - beta_one) * scaled
    second_new = beta_two * second + (1.0 - beta_two) * scaled * scaled
    first_hat = first_new / (1.0 - beta_one**step_count)
    second_hat = second_new / (1.0 - beta_two**step_count)
    direction = first_hat / (jnp.sqrt(second_hat) + epsilon)
    freshened_values = master - learn_rate * (direction + shrink_factor * master)
    return (direction, freshened_values)


def body(core, hbm, vm, outs, sc):
    (att_h, cot_h, nxt_h, mp_h, op_h, sp_h, me_h, oe_h, se_h) = hbm
    (t_now, t_next, ecot) = vm
    (o_np, o_ne, o_dir, o_dire, o_mst, o_mste, o_norm) = outs
    s = sc
    pos = [lax.axis_index(a) for a in AXES]
    other = 1 - core
    first, count = MINE[core]
    ofirst, ocount = MINE[other]
    units = UNITS[core]
    eunit = EUNIT[core]

    def at(axis, d):
        spot = list(pos)
        spot[axis] = lax.rem(pos[axis] + d, 4)
        return spot

    def in_plane(q, a, b):
        i, j = [k for k in range(3) if k != q]
        spot = list(pos)
        spot[i] = lax.rem(pos[i] + a, 4)
        spot[j] = lax.rem(pos[j] + b, 4)
        return spot

    def plane_of(q, spot):
        return [spot[k] for k in range(3) if k != q]

    def cut(q, p):
        index = [slice(None)] * 3
        index[q] = p
        return tuple(index)

    partner = tuple(pos[:3]) + (other,)

    def remote(src, dst, send, recv, spot):
        copy = pltpu.make_async_remote_copy(
            src_ref=src, dst_ref=dst, send_sem=send, recv_sem=recv,
            device_id=tuple(spot), device_id_type=MESH,
        )
        copy.start()

    def got(ref, sem):
        pltpu.make_async_remote_copy(
            src_ref=ref, dst_ref=ref, send_sem=sem, recv_sem=sem,
            device_id=partner, device_id_type=MESH,
        ).wait_recv()

    loads = []
    for k, (src, dst) in enumerate((
        (att_h, s.att), (cot_h, s.cot), (mp_h, s.st.at[core, 0]), (op_h, s.st.at[core, 1]),
        (sp_h, s.st.at[core, 2]), (me_h, s.ste.at[core, 0]), (oe_h, s.ste.at[core, 1]),
        (se_h, s.ste.at[core, 2]), (nxt_h, s.nxt),
    )):
        copy = pltpu.make_async_copy(src, dst, s.load_sem.at[k])
        copy.start()
        loads.append(copy)

    barrier = pltpu.get_barrier_semaphore()
    peers = {}
    for q in range(3):
        for a in range(4):
            for b in range(4):
                if (a, b) != (0, 0):
                    key = [0, 0, 0]
                    i, j = [k for k in range(3) if k != q]
                    key[i], key[j] = a, b
                    peers[tuple(key)] = in_plane(q, a, b)
    everyone = [tuple(p) for _, p in sorted(peers.items())] + [partner]
    for spot in everyone:
        pl.semaphore_signal(barrier, inc=1, device_id=spot, device_id_type=MESH)

    ladder = lax.broadcasted_iota(jnp.int32, (8, 128), 1).astype(F32)
    line = lax.broadcasted_iota(jnp.int32, (8, 128), 0)
    freqs = jnp.exp(-math.log(10000.0) * ladder / 128)
    moments = jnp.where(
        line == 0, t_now[0], jnp.where(line == 1, t_now[1], jnp.where(line == 2, t_next[0], t_next[1]))
    )
    phases = (moments * 1000.0) * freqs
    waves = jnp.concatenate([jnp.cos(phases), jnp.sin(phases)], axis=1).astype(BF16)
    columns = jnp.transpose(waves.astype(F32), (1, 0))

    loads[0].wait()
    s.attT[...] = jnp.transpose(s.att[...], (1, 0))
    loads[1].wait()

    def term(t):
        return jnp.dot(s.attT[...], s.cot[:, t * 128 : t * 128 + 128], preferred_element_type=F32)

    cots = ecot[...].astype(F32)

    def eterm(t):
        c = cots[:, t * 128 : t * 128 + 128]
        return columns[:, 0:1] * c[0:1] + columns[:, 1:2] * c[1:2]

    for j in range(ocount):
        s.psE[j] = eterm(ofirst + j).astype(BF16)
    pl.semaphore_wait(barrier, len(everyone))
    for k, src in enumerate((mp_h, op_h, sp_h)):
        remote(src, s.st.at[core, k], s.dsend.at[k], s.drecv.at[k], partner)
    for k, src in enumerate((me_h, oe_h, se_h)):
        remote(src, s.ste.at[core, k], s.dsend.at[3 + k], s.drecv.at[3 + k], partner)
    remote(s.psE.at[pl.ds(0, ocount)], s.prE.at[pl.ds(0, ocount)], s.dsend.at[6], s.drecv.at[6], partner)
    for j in range(ocount):
        s.ps[j] = term(ofirst + j).astype(BF16)
        remote(s.ps.at[j], s.pr.at[j], s.psend.at[j], s.precv.at[j], partner)
    for j in range(count):
        s.acc[j] = term(first + j)

    x2 = s.x.reshape(SLOTS, 1152, 128)
    xe2 = s.xE.reshape(SLOTS, 256, 128)

    def stage_one(u, x, r1, q, j0, n):
        for d in (1, 2, 3):
            spot = at(q, d)
            remote(
                x.at[(pl.ds(j0, n),) + cut(q, spot[q])],
                r1.at[pl.ds(j0, n), d],
                s.send1.at[u], s.recv1.at[u], spot,
            )
        for j in range(j0, j0 + n):
            r1[j, 0] = x[(j,) + cut(q, pos[q])]

    got(s.prE.at[pl.ds(0, count)], s.drecv.at[6])
    for j in range(count):
        xe2[j] = (eterm(first + j) + s.prE[j].astype(F32)).astype(BF16)
    stage_one(3, s.xE, s.r1E, *eunit)
    for u, (q, j0, n) in enumerate(units):
        for j in range(j0, j0 + n):
            got(s.pr.at[j], s.precv.at[j])
            x2[j] = (s.acc[j] + s.pr[j].astype(F32)).astype(BF16)
        stage_one(u, s.x, s.r1, q, j0, n)

    for k in range(6):
        loads[2 + k].wait()
    for k in range(3):
        got(s.st.at[other, k], s.drecv.at[k])
        got(s.ste.at[other, k], s.drecv.at[3 + k])
    for k in range(3):
        for j in range(count):
            t = first + j
            for half in range(2):
                s.reg[k, j, 9 * half : 9 * half + 9] = s.st[half, k, pl.ds(t, 9, stride=9), :]
                s.regE[k, j, 2 * half : 2 * half + 2] = s.ste[half, k, pl.ds(t, 2, stride=9), :]

    r1v = s.r1.reshape(SLOTS, 4, 288, 128)
    y2 = s.y.reshape(SLOTS, 288, 128)
    r1ve = s.r1E.reshape(SLOTS, 4, 64, 128)
    y2e = s.yE.reshape(SLOTS, 64, 128)

    def stage_two(u, r1, r1v, y, y2, r2, words, q, j0, n):
        got(r1.at[pl.ds(j0, n), pl.ds(1, 3)], s.recv1.at[u])
        for j in range(j0, j0 + n):
            total = r1v[j, 0].astype(F32)
            for d in (1, 2, 3):
                total = total + r1v[j, d].astype(F32)
            y2[j] = total.astype(BF16)
        for a in range(4):
            for b in range(4):
                if (a, b) == (0, 0):
                    continue
                spot = in_plane(q, a, b)
                p1, p2 = plane_of(q, spot)
                remote(
                    y.at[pl.ds(j0, n), p1, p2],
                    r2.at[pl.ds(j0, n), a * 4 + b, pl.ds(0, words)],
                    s.send2.at[u], s.recv2.at[u], spot,
                )
        p1, p2 = plane_of(q, pos)
        for j in range(j0, j0 + n):
            r2[j, 0, 0:words] = y[j, p1, p2]

    stage_two(3, s.r1E, r1ve, s.yE, y2e, s.r2E, 2, *eunit)
    for u, unit in enumerate(units):
        stage_two(u, s.r1, r1v, s.y, y2, s.r2, 9, *unit)

    r2v = s.r2.reshape(SLOTS, 16, 24, 128)
    r2ve = s.r2E.reshape(SLOTS, 16, 8, 128)
    squares = jnp.zeros((24, 128), F32)
    squares_e = jnp.zeros((8, 128), F32)

    q, j0, n = eunit
    got(s.r2E.at[pl.ds(j0, n), pl.ds(1, 15), pl.ds(0, 2)], s.recv2.at[3])
    for j in range(j0, j0 + n):
        total = r2ve[j, 0].astype(F32)
        for k in range(1, 16):
            total = total + r2ve[j, k].astype(F32)
        s.gE[j] = total
        squares_e = squares_e + total * total
    for u, (q, j0, n) in enumerate(units):
        got(s.r2.at[pl.ds(j0, n), pl.ds(1, 15), pl.ds(0, 9)], s.recv2.at[u])
        for j in range(j0, j0 + n):
            total = r2v[j, 0].astype(F32)
            for k in range(1, 16):
                total = total + r2v[j, k].astype(F32)
            s.g[j] = total
            squares = squares + total * total

    rows = lax.broadcasted_iota(jnp.int32, (24, 128), 0)
    rows_e = lax.broadcasted_iota(jnp.int32, (8, 128), 0)
    squares = jnp.sum(jnp.where(rows < 18, squares, 0.0), axis=0, keepdims=True)
    squares = squares + jnp.sum(jnp.where(rows_e < 4, squares_e, 0.0), axis=0, keepdims=True)
    s.na[core] = squares
    remote(s.na.at[core], s.na.at[core], s.nsend.at[0], s.nrecv.at[0], partner)
    got(s.na.at[other], s.nrecv.at[0])
    pz, py, px = pos[:3]
    s.nb[pz, py] = s.na[0] + s.na[1]
    for a in range(4):
        for b in range(4):
            if (a, b) != (0, 0):
                remote(s.nb.at[pz, py], s.nb.at[pz, py], s.nsend.at[1], s.nrecv.at[1], in_plane(2, a, b))
    got(s.nw.at[pl.ds(0, 15)], s.nrecv.at[1])
    total = s.nb[0, 0]
    for k in range(1, 16):
        total = total + s.nb[k // 4, k % 4]
    s.nc[px] = total
    for d in (1, 2, 3):
        remote(s.nc.at[px], s.nc.at[px], s.nsend.at[2], s.nrecv.at[2], at(2, d))
    got(s.nw.at[pl.ds(0, 3)], s.nrecv.at[2])
    total = s.nc[0] + s.nc[1] + s.nc[2] + s.nc[3]
    grad_norm = jnp.sqrt(jnp.sum(total, axis=1, keepdims=True))
    clip = jnp.minimum(jnp.float32(1.0), max_norm / (grad_norm + 1e-06))
    o_norm[...] = jnp.broadcast_to(grad_norm, (1, 128))

    z2 = s.zz.reshape(SLOTS, 24, 128)
    z2e = s.zE.reshape(SLOTS, 8, 128)

    def update(u, g, reg, zz, z2, dirs, v, words, q, j0, n):
        for j in range(j0, j0 + n):
            direction, fresh = adamw_update(g[j], clip, reg[0, j], reg[1, j], reg[2, j])
            dirs[0, j] = direction
            dirs[1, j] = fresh
            z2[j] = fresh.astype(BF16)
        p1, p2 = plane_of(q, pos)
        for a in range(4):
            for b in range(4):
                if (a, b) == (0, 0):
                    continue
                remote(
                    zz.at[pl.ds(j0, n), pl.ds(0, words)],
                    v.at[pl.ds(j0, n), p1, p2],
                    s.send3.at[u], s.recv3.at[u], in_plane(q, a, b),
                )
        for j in range(j0, j0 + n):
            v[j, p1, p2] = zz[j, 0:words]

    for u, unit in enumerate(units):
        update(u, s.g, s.reg, s.zz, z2, s.dirs, s.v, 9, *unit)
    update(3, s.gE, s.regE, s.zE, z2e, s.dirsE, s.vE, 2, *eunit)

    for k in range(2):
        for j in range(count):
            s.os[k, j, 0:9] = s.dirs[k, j, 9 * other : 9 * other + 9]
            s.osE[k, j, 0:2] = s.dirsE[k, j, 2 * other : 2 * other + 2]
    remote(s.os, s.orr, s.dsend.at[7], s.drecv.at[7], partner)
    remote(s.osE, s.orrE, s.dsend.at[8], s.drecv.at[8], partner)
    for k, (out, oute) in enumerate(((o_dir, o_dire), (o_mst, o_mste))):
        for j in range(count):
            out[pl.ds(first + j, 9, stride=9), :] = s.dirs[k, j, 9 * core : 9 * core + 9]
            oute[pl.ds(first + j, 2, stride=9), :] = s.dirsE[k, j, 2 * core : 2 * core + 2]

    def ring(u, r2, v, w, words, q, j0, n):
        got(r2.at[pl.ds(j0, n), pl.ds(1, 15), pl.ds(0, words)], s.recv3.at[u])
        for d in (1, 2, 3):
            remote(
                v.at[pl.ds(j0, n)],
                w.at[(pl.ds(first + j0, n),) + cut(q, pos[q])],
                s.send4.at[u], s.recv4.at[u], at(q, d),
            )
        for j in range(j0, j0 + n):
            w[(first + j,) + cut(q, pos[q])] = v[j]

    for u, unit in enumerate(units):
        ring(u, s.r2, s.v, s.w, 9, *unit)
    ring(3, s.r2E, s.vE, s.wE, 2, *eunit)

    got(s.orr, s.drecv.at[7])
    got(s.orrE, s.drecv.at[8])
    for k, (out, oute) in enumerate(((o_dir, o_dire), (o_mst, o_mste))):
        for j in range(ocount):
            out[pl.ds(ofirst + j, 9, stride=9), :] = s.orr[k, j, 0:9]
            oute[pl.ds(ofirst + j, 2, stride=9), :] = s.orrE[k, j, 0:2]

    loads[8].wait()
    w2 = s.w.reshape(TILES, 1152, 128)
    we2 = s.wE.reshape(TILES, 256, 128)

    def product(t):
        o_np[:, t * 128 : t * 128 + 128] = jnp.dot(
            s.nxt[...], w2[t], preferred_element_type=F32
        ).astype(BF16)

    for u, (q, j0, n) in enumerate(units):
        got(s.r1.at[pl.ds(j0, n), pl.ds(1, 3)], s.recv4.at[u])
        whole = s.w.at[pl.ds(first + j0, n)]
        remote(whole, whole, s.send5.at[u], s.recv5.at[u], partner)
        for j in range(j0, j0 + n):
            product(first + j)
    q, j0, n = eunit
    got(s.r1E.at[pl.ds(j0, n), pl.ds(1, 3)], s.recv4.at[3])
    whole = s.wE.at[pl.ds(first, count)]
    remote(whole, whole, s.send5.at[3], s.recv5.at[3], partner)
    for u, (q, j0, n) in enumerate(UNITS[other]):
        got(s.w.at[pl.ds(ofirst + j0, n)], s.recv5.at[u])
        for j in range(j0, j0 + n):
            product(ofirst + j)
    got(s.wE.at[pl.ds(ofirst, ocount)], s.recv5.at[3])
    for t in range(TILES):
        mixed = jnp.dot(waves, we2[t], preferred_element_type=F32)
        o_ne[:, t * 128 : t * 128 + 128] = mixed[2:4].astype(BF16)

    def sent(ref, sem):
        pltpu.make_async_remote_copy(
            src_ref=ref, dst_ref=ref, send_sem=sem, recv_sem=sem,
            device_id=partner, device_id_type=MESH,
        ).wait_send()

    for k in range(3):
        sent(s.st.at[core, k], s.dsend.at[k])
        sent(s.ste.at[core, k], s.dsend.at[3 + k])
    sent(s.psE.at[pl.ds(0, ocount)], s.dsend.at[6])
    sent(s.os, s.dsend.at[7])
    sent(s.osE, s.dsend.at[8])
    for j in range(ocount):
        sent(s.ps.at[j], s.psend.at[j])
    sent(s.na.at[core], s.nsend.at[0])
    sent(s.nw.at[pl.ds(0, 15)], s.nsend.at[1])
    sent(s.nw.at[pl.ds(0, 3)], s.nsend.at[2])
    for u, (q, j0, n) in enumerate(units):
        sent(s.r1.at[pl.ds(j0, n), pl.ds(1, 3)], s.send1.at[u])
        sent(s.r2.at[pl.ds(j0, n), pl.ds(1, 15), pl.ds(0, 9)], s.send2.at[u])
        sent(s.r2.at[pl.ds(j0, n), pl.ds(1, 15), pl.ds(0, 9)], s.send3.at[u])
        sent(s.r1.at[pl.ds(j0, n), pl.ds(1, 3)], s.send4.at[u])
        sent(s.w.at[pl.ds(first + j0, n)], s.send5.at[u])
    q, j0, n = eunit
    sent(s.r1E.at[pl.ds(j0, n), pl.ds(1, 3)], s.send1.at[3])
    sent(s.r2E.at[pl.ds(j0, n), pl.ds(1, 15), pl.ds(0, 2)], s.send2.at[3])
    sent(s.r2E.at[pl.ds(j0, n), pl.ds(1, 15), pl.ds(0, 2)], s.send3.at[3])
    sent(s.r1E.at[pl.ds(j0, n), pl.ds(1, 3)], s.send4.at[3])
    sent(s.wE.at[pl.ds(first, count)], s.send5.at[3])


class Names:
    pass


DMA = pltpu.SemaphoreType.DMA
SCRATCH = dict(
    att=pltpu.VMEM((512, 1152), BF16),
    cot=pltpu.VMEM((512, 1152), BF16),
    nxt=pltpu.VMEM((512, 1152), BF16),
    attT=pltpu.VMEM((1152, 512), BF16),
    st=pltpu.VMEM((2, 3, 81, 128), F32),
    ste=pltpu.VMEM((2, 3, 18, 128), F32),
    ps=pltpu.VMEM((SLOTS, 1152, 128), BF16),
    pr=pltpu.VMEM((SLOTS, 1152, 128), BF16),
    psE=pltpu.VMEM((SLOTS, 256, 128), BF16),
    prE=pltpu.VMEM((SLOTS, 256, 128), BF16),
    acc=pltpu.VMEM((SLOTS, 1152, 128), F32),
    x=pltpu.VMEM((SLOTS, 4, 4, 4, 9, 2, 128), BF16),
    xE=pltpu.VMEM((SLOTS, 4, 4, 4, 2, 2, 128), BF16),
    r1=pltpu.VMEM((SLOTS, 4, 4, 4, 9, 2, 128), BF16),
    r1E=pltpu.VMEM((SLOTS, 4, 4, 4, 2, 2, 128), BF16),
    y=pltpu.VMEM((SLOTS, 4, 4, 9, 2, 128), BF16),
    yE=pltpu.VMEM((SLOTS, 4, 4, 2, 2, 128), BF16),
    r2=pltpu.VMEM((SLOTS, 16, 12, 2, 128), BF16),
    r2E=pltpu.VMEM((SLOTS, 16, 4, 2, 128), BF16),
    reg=pltpu.VMEM((3, SLOTS, 24, 128), F32),
    regE=pltpu.VMEM((3, SLOTS, 8, 128), F32),
    g=pltpu.VMEM((SLOTS, 24, 128), F32),
    gE=pltpu.VMEM((SLOTS, 8, 128), F32),
    dirs=pltpu.VMEM((2, SLOTS, 24, 128), F32),
    dirsE=pltpu.VMEM((2, SLOTS, 8, 128), F32),
    zz=pltpu.VMEM((SLOTS, 12, 2, 128), BF16),
    zE=pltpu.VMEM((SLOTS, 4, 2, 128), BF16),
    v=pltpu.VMEM((SLOTS, 4, 4, 9, 2, 128), BF16),
    vE=pltpu.VMEM((SLOTS, 4, 4, 2, 2, 128), BF16),
    w=pltpu.VMEM((TILES, 4, 4, 4, 9, 2, 128), BF16),
    wE=pltpu.VMEM((TILES, 4, 4, 4, 2, 2, 128), BF16),
    os=pltpu.VMEM((2, SLOTS, 16, 128), F32),
    osE=pltpu.VMEM((2, SLOTS, 8, 128), F32),
    orr=pltpu.VMEM((2, SLOTS, 16, 128), F32),
    orrE=pltpu.VMEM((2, SLOTS, 8, 128), F32),
    na=pltpu.VMEM((2, 1, 128), F32),
    nb=pltpu.VMEM((4, 4, 1, 128), F32),
    nc=pltpu.VMEM((4, 1, 128), F32),
    nw=pltpu.VMEM((15, 1, 128), F32),
    load_sem=DMA((9,)),
    dsend=DMA((9,)),
    drecv=DMA((9,)),
    psend=DMA((SLOTS,)),
    precv=DMA((SLOTS,)),
    send1=DMA((4,)),
    recv1=DMA((4,)),
    send2=DMA((4,)),
    recv2=DMA((4,)),
    send3=DMA((4,)),
    recv3=DMA((4,)),
    send4=DMA((4,)),
    recv4=DMA((4,)),
    send5=DMA((4,)),
    recv5=DMA((4,)),
    nsend=DMA((3,)),
    nrecv=DMA((3,)),
)


def kernel(*refs):
    hbm, vm, outs, scratch = refs[:9], refs[9:12], refs[12:19], refs[19:]
    s = Names()
    for name, ref in zip(SCRATCH, scratch, strict=True):
        setattr(s, name, ref)
    core = lax.axis_index("c")
    for k in (0, 1):

        @pl.when(core == k)
        def _():
            body(k, hbm, vm, outs, s)


def shards(
    attended, proj_cot, timesteps, embed_cot, master_proj, moment_proj, second_proj,
    master_embed, moment_embed, squared_moment_layer, attended_next, timesteps_next,
):
    flat = [a.reshape(-1, 128) for a in (master_proj, moment_proj, second_proj)]
    flat_e = [a.reshape(-1, 128) for a in (master_embed, moment_embed, squared_moment_layer)]
    anywhere = pl.BlockSpec(memory_space=pl.ANY)
    smem = pl.BlockSpec(memory_space=pltpu.SMEM)
    vmem = pl.BlockSpec(memory_space=pltpu.VMEM)
    shape = jax.ShapeDtypeStruct
    nproj, nembed, d, de, m, mste, norm = pl.pallas_call(
        kernel,
        out_shape=(
            shape((512, 1152), BF16), shape((2, 1152), BF16), shape((81, 128), F32),
            shape((18, 128), F32), shape((81, 128), F32), shape((18, 128), F32), shape((1, 128), F32),
        ),
        in_specs=[anywhere] * 9 + [smem, smem, vmem],
        out_specs=[vmem] * 7,
        scratch_shapes=list(SCRATCH.values()),
        compiler_params=pltpu.CompilerParams(
            collective_id=0, has_side_effects=True, vmem_limit_bytes=48 * 2**20
        ),
    )(attended, proj_cot, attended_next, *flat, *flat_e, timesteps, timesteps_next, embed_cot)
    return (
        nproj, nembed, d.reshape(-1), de.reshape(-1), m.reshape(-1), mste.reshape(-1), norm[0, 0],
    )


def solution(mesh):
    finer = Mesh(mesh.devices.reshape(4, 4, 4, 2), AXES)
    dp = P(AXES)
    wide = P(AXES, None)
    return jax.shard_map(
        shards,
        mesh=finer,
        in_specs=(wide, wide, dp, wide, dp, dp, dp, dp, dp, dp, wide, dp),
        out_specs=(wide, wide, dp, dp, dp, dp, P()),
        check_vma=False,
    )
```

time: 317 us -> 73.7 us (0.23)
  waiting for transfers between devices: 227 us -> 0 us
  Pallas kernels: 0 us -> 57 us
  blocking collectives: 33.5 us -> 0 us
  between operations: 17.3 us -> 1.83 us
  matrix products: 9.74 us -> 0 us
  local copies, waits for them, and re-layouts: 21.8 us -> 14.3 us
  other arithmetic: 6.77 us -> 0 us
    unnamed x3 -> x0, waiting for transfers between devices: 163 us -> none
    all_gather x1 -> x0, waiting for transfers between devices: 63.9 us -> none  [gather_packed(): lines, at, finished = (lax.all_gather(flat, axis), 0, [])]
    pallas_call x0 -> x1, Pallas kernels: none -> 57 us  [shards(): pl.pallas_call(kernel, out_shape=(shape((512, 1152), BF16), shape((2, 115...]
    psum x4 -> x0, blocking collectives: 33.5 us -> none  [over_axes(): value = lax.psum(value, axis)]
    dot_general x4 -> x0, matrix products: 9.74 us -> none  [the longest x1 4.08 us: shards(): jnp.dot(attended.T, proj_cot, preferred_element_type=jnp.float32)]
    unnamed x19 -> x30, local copies, waits for them, and re-layouts: 5.88 us -> 14.3 us
    reshape x2 -> x0, local copies, waits for them, and re-layouts: 7.64 us -> none  [the longest x1 6.55 us: shards(): jnp.dot(attended.T, proj_cot, preferred_element_type=jnp.float32)]
    another operation x2 -> x0, local copies, waits for them, and re-layouts: 6.56 us -> none  [the longest x1 6.36 us: shards(): weight_proj = whole_proj.reshape(width, width)]
  transfers between devices with their start and end apart: 2 -> 0, of which waited for: 2 -> 0; matrix products, arithmetic and copies ran while one was open for 0% -> 0% of each run, Pallas kernels for 0% -> 0%
where the time goes in v1:
time: 73.7 us; the launch traced here: 73.1 us
  Pallas kernels  57 us (77%)
  local copies, waits for them, and re-layouts  14.3 us (19%)
  between operations  1.83 us (2%)
    pallas_call x1, Pallas kernels, shards(): pl.pallas_call(kernel, out_shape=(shape((512, 1152), BF16), shape((2, 115...  57 us
    unnamed x30, local copies, waits for them, and re-layouts  14.3 us

profile of v1, /device:TPU:1, one launch (start us, length us, event | category | flops | bytes accessed | tf_op | source)
XLA Modules:
  0.0 73.1 jit_solution(9986682687579432740)
XLA Ops:
  0.6 0.0 copy-start
  0.6 1.3 %copy-done = bf16[512,1152]{1,0:T(8,128)(2,1)S(1)} copy-done((bf16[512,1152]{1,0:T(8,128)(2,1)S(1)}, bf16[512,1152]{1,0:T(8,128)(2,1)}, u32[]{:S(2)}) %copy-start) | copy-done | bytes 1179672
  1.9 0.0 copy-start.1
  1.9 1.3 %copy-done.1 = bf16[512,1152]{1,0:T(8,128)(2,1)S(1)} copy-done((bf16[512,1152]{1,0:T(8,128)(2,1)S(1)}, bf16[512,1152]{1,0:T(8,128)(2,1)}, u32[]{:S(2)}) %copy-start.1) | copy-done | bytes 1179672
  3.2 0.0 copy-start.2
  3.2 1.3 %copy-done.2 = bf16[512,1152]{1,0:T(8,128)(2,1)S(1)} copy-done((bf16[512,1152]{1,0:T(8,128)(2,1)S(1)}, bf16[512,1152]{1,0:T(8,128)(2,1)}, u32[]{:S(2)}) %copy-start.2) | copy-done | bytes 1179672
  4.5 0.0 copy-start.3
  4.5 0.8 %copy-done.3 = f32[10368]{0:T(1024)S(1)} copy-done((f32[10368]{0:T(1024)S(1)}, f32[10368]{0:T(1024)}, u32[]{:S(2)}) %copy-start.3) | copy-done | bytes 41496
  5.2 0.0 copy-start.4
  5.2 0.8 %copy-done.4 = f32[10368]{0:T(1024)S(1)} copy-done((f32[10368]{0:T(1024)S(1)}, f32[10368]{0:T(1024)}, u32[]{:S(2)}) %copy-start.4) | copy-done | bytes 41496
  6.0 0.0 copy-start.5
  6.0 0.8 %copy-done.5 = f32[10368]{0:T(1024)S(1)} copy-done((f32[10368]{0:T(1024)S(1)}, f32[10368]{0:T(1024)}, u32[]{:S(2)}) %copy-start.5) | copy-done | bytes 41496
  6.8 0.0 copy-start.6
  6.8 0.7 copy-done.6
  7.5 0.0 copy-start.7
  7.5 0.7 copy-done.7
  8.2 0.0 copy-start.8
  8.2 0.7 copy-done.8
  8.9 0.0 copy-start.9
  8.9 0.7 copy-done.9
  9.6 0.0 copy-start.10
  9.6 0.7 copy-done.10
  10.3 0.0 copy-start.11
  10.3 0.7 copy-done.11
  10.9 57.0 %shard_map.171 = (bf16[512,1152]{1,0:T(8,128)(2,1)S(1)}, bf16[2,1152]{1,0:T(2,128)(2,1)S(1)}, f32[81,128]{1,0:T(8,128)S(1)}, f32[18,128]{1,0:T(8,128)S(1)}, f32[...) custom-call(bf16[512,1152]{1,0:T(8,128)(2,1)S(1)} %copy-done, bf16[512,1152]{1,0:T(8,128)(2,1)S(1)} %copy-done.1, ...), custom_call_target="tpu_custom_call" | custom-call | tf_op jit(solution)/shard_map/pallas_call | solution.py:475
  67.9 1.0 %copy.26 = bf16[512,1152]{1,0:T(8,128)(2,1)} copy(bf16[512,1152]{1,0:T(8,128)(2,1)S(1)} %get-tuple-element.28) | data formatting | bytes 2359296
  68.9 0.6 copy.27
  69.5 0.6 copy.28
  70.1 0.6 copy.29
  70.7 0.6 copy.30
  71.4 0.6 copy.31
Async XLA Ops:
  0.6 1.3 %copy-start = (bf16[512,1152]{1,0:T(8,128)(2,1)S(1)}, bf16[512,1152]{1,0:T(8,128)(2,1)}, u32[]{:S(2)}) copy-start(bf16[512,1152]{1,0:T(8,128)(2,1)} %refs_0_.1) | copy-start | bytes 3538948
  1.9 1.3 %copy-start.1 = (bf16[512,1152]{1,0:T(8,128)(2,1)S(1)}, bf16[512,1152]{1,0:T(8,128)(2,1)}, u32[]{:S(2)}) copy-start(bf16[512,1152]{1,0:T(8,128)(2,1)} %refs_1_.1) | copy-start | bytes 3538948
  3.2 1.3 %copy-start.2 = (bf16[512,1152]{1,0:T(8,128)(2,1)S(1)}, bf16[512,1152]{1,0:T(8,128)(2,1)}, u32[]{:S(2)}) copy-start(bf16[512,1152]{1,0:T(8,128)(2,1)} %refs_2_.1) | copy-start | bytes 3538948
  4.5 0.8 %copy-start.3 = (f32[10368]{0:T(1024)S(1)}, f32[10368]{0:T(1024)}, u32[]{:S(2)}) copy-start(f32[10368]{0:T(1024)} %param.16) | copy-start | bytes 124420
  5.2 0.8 %copy-start.4 = (f32[10368]{0:T(1024)S(1)}, f32[10368]{0:T(1024)}, u32[]{:S(2)}) copy-start(f32[10368]{0:T(1024)} %param.17) | copy-start | bytes 124420
  6.0 0.8 %copy-start.5 = (f32[10368]{0:T(1024)S(1)}, f32[10368]{0:T(1024)}, u32[]{:S(2)}) copy-start(f32[10368]{0:T(1024)} %param.18) | copy-start | bytes 124420
  6.8 0.7 copy-start.6
  7.5 0.7 copy-start.7
  8.2 0.7 copy-start.8
  8.9 0.7 copy-start.9
  9.6 0.7 copy-start.10
  10.3 0.7 copy-start.11

commit v2 on v1

--- a/solution.py
+++ b/solution.py
@@ -30,6 +30,7 @@
 }
 EUNIT = {0: (2, 0, 5), 1: (0, 0, 4)}
 SLOTS = 5
+PHASES = False
 
 
 def adamw_update(gradient, clip, master, moment, second):
@@ -43,9 +44,8 @@
     return (direction, freshened_values)
 
 
-def body(core, hbm, vm, outs, sc):
-    (att_h, cot_h, nxt_h, mp_h, op_h, sp_h, me_h, oe_h, se_h) = hbm
-    (t_now, t_next, ecot) = vm
+def body(core, hbm, outs, sc):
+    (att_h, cot_h, nxt_h, mp_h, op_h, sp_h, me_h, oe_h, se_h, tn_h, tx_h, ec_h) = hbm
     (o_np, o_ne, o_dir, o_dire, o_mst, o_mste, o_norm) = outs
     s = sc
     pos = [lax.axis_index(a) for a in AXES]
@@ -90,16 +90,19 @@
             device_id=partner, device_id_type=MESH,
         ).wait_recv()
 
+    phase = Phase()
+    phase("start")
     loads = []
     for k, (src, dst) in enumerate((
         (att_h, s.att), (cot_h, s.cot), (mp_h, s.st.at[core, 0]), (op_h, s.st.at[core, 1]),
         (sp_h, s.st.at[core, 2]), (me_h, s.ste.at[core, 0]), (oe_h, s.ste.at[core, 1]),
-        (se_h, s.ste.at[core, 2]), (nxt_h, s.nxt),
+        (se_h, s.ste.at[core, 2]), (nxt_h, s.nxt), (tn_h, s.now), (tx_h, s.later), (ec_h, s.ecot),
     )):
         copy = pltpu.make_async_copy(src, dst, s.load_sem.at[k])
         copy.start()
         loads.append(copy)
 
+    phase("signal")
     barrier = pltpu.get_barrier_semaphore()
     peers = {}
     for q in range(3):
@@ -114,6 +117,10 @@
     for spot in everyone:
         pl.semaphore_signal(barrier, inc=1, device_id=spot, device_id_type=MESH)
 
+    phase("freqs")
+    for k in (9, 10, 11):
+        loads[k].wait()
+    t_now, t_next, ecot = s.now, s.later, s.ecot
     ladder = lax.broadcasted_iota(jnp.int32, (8, 128), 1).astype(F32)
     line = lax.broadcasted_iota(jnp.int32, (8, 128), 0)
     freqs = jnp.exp(-math.log(10000.0) * ladder / 128)
@@ -124,10 +131,12 @@
     waves = jnp.concatenate([jnp.cos(phases), jnp.sin(phases)], axis=1).astype(BF16)
     columns = jnp.transpose(waves.astype(F32), (1, 0))
 
+    phase("transpose")
     loads[0].wait()
     s.attT[...] = jnp.transpose(s.att[...], (1, 0))
     loads[1].wait()
 
+    phase("eterms")
     def term(t):
         return jnp.dot(s.attT[...], s.cot[:, t * 128 : t * 128 + 128], preferred_element_type=F32)
 
@@ -139,7 +148,9 @@
 
     for j in range(ocount):
         s.psE[j] = eterm(ofirst + j).astype(BF16)
+    phase("barrier")
     pl.semaphore_wait(barrier, len(everyone))
+    phase("partner_terms")
     for k, src in enumerate((mp_h, op_h, sp_h)):
         remote(src, s.st.at[core, k], s.dsend.at[k], s.drecv.at[k], partner)
     for k, src in enumerate((me_h, oe_h, se_h)):
@@ -148,6 +159,7 @@
     for j in range(ocount):
         s.ps[j] = term(ofirst + j).astype(BF16)
         remote(s.ps.at[j], s.pr.at[j], s.psend.at[j], s.precv.at[j], partner)
+    phase("own_terms")
     for j in range(count):
         s.acc[j] = term(first + j)
 
@@ -165,16 +177,19 @@
         for j in range(j0, j0 + n):
             r1[j, 0] = x[(j,) + cut(q, pos[q])]
 
+    phase("chip_e")
     got(s.prE.at[pl.ds(0, count)], s.drecv.at[6])
     for j in range(count):
         xe2[j] = (eterm(first + j) + s.prE[j].astype(F32)).astype(BF16)
     stage_one(3, s.xE, s.r1E, *eunit)
     for u, (q, j0, n) in enumerate(units):
+        phase(f"chip{u}")
         for j in range(j0, j0 + n):
             got(s.pr.at[j], s.precv.at[j])
             x2[j] = (s.acc[j] + s.pr[j].astype(F32)).astype(BF16)
         stage_one(u, s.x, s.r1, q, j0, n)
 
+    phase("state")
     for k in range(6):
         loads[2 + k].wait()
     for k in range(3):
@@ -214,8 +229,10 @@
         for j in range(j0, j0 + n):
             r2[j, 0, 0:words] = y[j, p1, p2]
 
+    phase("two_e")
     stage_two(3, s.r1E, r1ve, s.yE, y2e, s.r2E, 2, *eunit)
     for u, unit in enumerate(units):
+        phase(f"two{u}")
         stage_two(u, s.r1, r1v, s.y, y2, s.r2, 9, *unit)
 
     r2v = s.r2.reshape(SLOTS, 16, 24, 128)
@@ -223,6 +240,7 @@
     squares = jnp.zeros((24, 128), F32)
     squares_e = jnp.zeros((8, 128), F32)
 
+    phase("sum_e")
     q, j0, n = eunit
     got(s.r2E.at[pl.ds(j0, n), pl.ds(1, 15), pl.ds(0, 2)], s.recv2.at[3])
     for j in range(j0, j0 + n):
@@ -232,6 +250,7 @@
         s.gE[j] = total
         squares_e = squares_e + total * total
     for u, (q, j0, n) in enumerate(units):
+        phase(f"sum{u}")
         got(s.r2.at[pl.ds(j0, n), pl.ds(1, 15), pl.ds(0, 9)], s.recv2.at[u])
         for j in range(j0, j0 + n):
             total = r2v[j, 0].astype(F32)
@@ -240,12 +259,14 @@
             s.g[j] = total
             squares = squares + total * total
 
+    phase("squares")
     rows = lax.broadcasted_iota(jnp.int32, (24, 128), 0)
     rows_e = lax.broadcasted_iota(jnp.int32, (8, 128), 0)
     squares = jnp.sum(jnp.where(rows < 18, squares, 0.0), axis=0, keepdims=True)
     squares = squares + jnp.sum(jnp.where(rows_e < 4, squares_e, 0.0), axis=0, keepdims=True)
     s.na[core] = squares
     remote(s.na.at[core], s.na.at[core], s.nsend.at[0], s.nrecv.at[0], partner)
+    phase("norm_a")
     got(s.na.at[other], s.nrecv.at[0])
     pz, py, px = pos[:3]
     s.nb[pz, py] = s.na[0] + s.na[1]
@@ -253,6 +274,7 @@
         for b in range(4):
             if (a, b) != (0, 0):
                 remote(s.nb.at[pz, py], s.nb.at[pz, py], s.nsend.at[1], s.nrecv.at[1], in_plane(2, a, b))
+    phase("norm_b")
     got(s.nw.at[pl.ds(0, 15)], s.nrecv.at[1])
     total = s.nb[0, 0]
     for k in range(1, 16):
@@ -260,6 +282,7 @@
     s.nc[px] = total
     for d in (1, 2, 3):
         remote(s.nc.at[px], s.nc.at[px], s.nsend.at[2], s.nrecv.at[2], at(2, d))
+    phase("norm_c")
     got(s.nw.at[pl.ds(0, 3)], s.nrecv.at[2])
     total = s.nc[0] + s.nc[1] + s.nc[2] + s.nc[3]
     grad_norm = jnp.sqrt(jnp.sum(total, axis=1, keepdims=True))
@@ -288,10 +311,12 @@
         for j in range(j0, j0 + n):
             v[j, p1, p2] = zz[j, 0:words]
 
+    phase("update")
     for u, unit in enumerate(units):
         update(u, s.g, s.reg, s.zz, z2, s.dirs, s.v, 9, *unit)
     update(3, s.gE, s.regE, s.zE, z2e, s.dirsE, s.vE, 2, *eunit)
 
+    phase("outs")
     for k in range(2):
         for j in range(count):
             s.os[k, j, 0:9] = s.dirs[k, j, 9 * other : 9 * other + 9]
@@ -315,9 +340,12 @@
             w[(first + j,) + cut(q, pos[q])] = v[j]
 
     for u, unit in enumerate(units):
+        phase(f"ring{u}")
         ring(u, s.r2, s.v, s.w, 9, *unit)
+    phase("ring_e")
     ring(3, s.r2E, s.vE, s.wE, 2, *eunit)
 
+    phase("outs2")
     got(s.orr, s.drecv.at[7])
     got(s.orrE, s.drecv.at[8])
     for k, (out, oute) in enumerate(((o_dir, o_dire), (o_mst, o_mste))):
@@ -335,24 +363,29 @@
         ).astype(BF16)
 
     for u, (q, j0, n) in enumerate(units):
+        phase(f"own{u}")
         got(s.r1.at[pl.ds(j0, n), pl.ds(1, 3)], s.recv4.at[u])
         whole = s.w.at[pl.ds(first + j0, n)]
         remote(whole, whole, s.send5.at[u], s.recv5.at[u], partner)
         for j in range(j0, j0 + n):
             product(first + j)
+    phase("own_e")
     q, j0, n = eunit
     got(s.r1E.at[pl.ds(j0, n), pl.ds(1, 3)], s.recv4.at[3])
     whole = s.wE.at[pl.ds(first, count)]
     remote(whole, whole, s.send5.at[3], s.recv5.at[3], partner)
     for u, (q, j0, n) in enumerate(UNITS[other]):
+        phase(f"theirs{u}")
         got(s.w.at[pl.ds(ofirst + j0, n)], s.recv5.at[u])
         for j in range(j0, j0 + n):
             product(ofirst + j)
+    phase("last_e")
     got(s.wE.at[pl.ds(ofirst, ocount)], s.recv5.at[3])
     for t in range(TILES):
         mixed = jnp.dot(waves, we2[t], preferred_element_type=F32)
         o_ne[:, t * 128 : t * 128 + 128] = mixed[2:4].astype(BF16)
 
+    phase("drain")
     def sent(ref, sem):
         pltpu.make_async_remote_copy(
             src_ref=ref, dst_ref=ref, send_sem=sem, recv_sem=sem,
@@ -382,10 +415,24 @@
     sent(s.r2E.at[pl.ds(j0, n), pl.ds(1, 15), pl.ds(0, 2)], s.send3.at[3])
     sent(s.r1E.at[pl.ds(j0, n), pl.ds(1, 3)], s.send4.at[3])
     sent(s.wE.at[pl.ds(first, count)], s.send5.at[3])
+    phase(None)
 
 
 class Names:
     pass
+
+
+class Phase:
+    def __init__(self):
+        self.open = None
+
+    def __call__(self, name):
+        if self.open is not None:
+            self.open.__exit__(None, None, None)
+            self.open = None
+        if name is not None and PHASES:
+            self.open = jax.named_scope(name)
+            self.open.__enter__()
 
 
 DMA = pltpu.SemaphoreType.DMA
@@ -393,6 +440,9 @@
     att=pltpu.VMEM((512, 1152), BF16),
     cot=pltpu.VMEM((512, 1152), BF16),
     nxt=pltpu.VMEM((512, 1152), BF16),
+    ecot=pltpu.VMEM((2, 1152), BF16),
+    now=pltpu.SMEM((2,), F32),
+    later=pltpu.SMEM((2,), F32),
     attT=pltpu.VMEM((1152, 512), BF16),
     st=pltpu.VMEM((2, 3, 81, 128), F32),
     ste=pltpu.VMEM((2, 3, 18, 128), F32),
@@ -429,7 +479,7 @@
     nb=pltpu.VMEM((4, 4, 1, 128), F32),
     nc=pltpu.VMEM((4, 1, 128), F32),
     nw=pltpu.VMEM((15, 1, 128), F32),
-    load_sem=DMA((9,)),
+    load_sem=DMA((12,)),
     dsend=DMA((9,)),
     drecv=DMA((9,)),
     psend=DMA((SLOTS,)),
@@ -450,7 +500,7 @@
 
 
 def kernel(*refs):
-    hbm, vm, outs, scratch = refs[:9], refs[9:12], refs[12:19], refs[19:]
+    hbm, outs, scratch = refs[:12], refs[12:19], refs[19:]
     s = Names()
     for name, ref in zip(SCRATCH, scratch, strict=True):
         setattr(s, name, ref)
@@ -459,7 +509,16 @@
 
         @pl.when(core == k)
         def _():
-            body(k, hbm, vm, outs, s)
+            body(k, hbm, outs, s)
+
+
+def write_out(*refs):
+    sems = refs[14]
+    copies = [pltpu.make_async_copy(refs[k], refs[7 + k], sems.at[k]) for k in range(7)]
+    for copy in copies:
+        copy.start()
+    for copy in copies:
+        copy.wait()
 
 
 def shards(
@@ -469,22 +528,33 @@
     flat = [a.reshape(-1, 128) for a in (master_proj, moment_proj, second_proj)]
     flat_e = [a.reshape(-1, 128) for a in (master_embed, moment_embed, squared_moment_layer)]
     anywhere = pl.BlockSpec(memory_space=pl.ANY)
-    smem = pl.BlockSpec(memory_space=pltpu.SMEM)
+    large = pl.BlockSpec(memory_space=pltpu.HBM)
     vmem = pl.BlockSpec(memory_space=pltpu.VMEM)
     shape = jax.ShapeDtypeStruct
-    nproj, nembed, d, de, m, mste, norm = pl.pallas_call(
+    results = (
+        shape((512, 1152), BF16), shape((2, 1152), BF16), shape((81, 128), F32),
+        shape((18, 128), F32), shape((81, 128), F32), shape((18, 128), F32), shape((1, 128), F32),
+    )
+    inside = pl.pallas_call(
         kernel,
-        out_shape=(
-            shape((512, 1152), BF16), shape((2, 1152), BF16), shape((81, 128), F32),
-            shape((18, 128), F32), shape((81, 128), F32), shape((18, 128), F32), shape((1, 128), F32),
-        ),
-        in_specs=[anywhere] * 9 + [smem, smem, vmem],
+        out_shape=[pltpu.VMEM(r.shape, r.dtype) for r in results],
+        in_specs=[large] * 12,
         out_specs=[vmem] * 7,
         scratch_shapes=list(SCRATCH.values()),
         compiler_params=pltpu.CompilerParams(
-            collective_id=0, has_side_effects=True, vmem_limit_bytes=48 * 2**20
+            collective_id=0, has_side_effects=True, vmem_limit_bytes=60 * 2**20
         ),
+        name="step",
     )(attended, proj_cot, attended_next, *flat, *flat_e, timesteps, timesteps_next, embed_cot)
+    nproj, nembed, d, de, m, mste, norm = pl.pallas_call(
+        write_out,
+        out_shape=results,
+        in_specs=[vmem] * 7,
+        out_specs=[large] * 7,
+        scratch_shapes=[DMA((7,))],
+        compiler_params=pltpu.CompilerParams(vmem_limit_bytes=8 * 2**20),
+        name="write_out",
+    )(*inside)
     return (
         nproj, nembed, d.reshape(-1), de.reshape(-1), m.reshape(-1), mste.reshape(-1), norm[0, 0],
     )

time: 73.7 us -> 57.5 us (0.78)
  local copies, waits for them, and re-layouts: 14.3 us -> 0 us
  between operations: 1.83 us -> 0.81 us
    unnamed x30 -> x0, local copies, waits for them, and re-layouts: 14.3 us -> none
    pallas_call x1 -> x2, Pallas kernels: 57 us -> 56.5 us  [the longest x1 55.4 us: shards(): pl.pallas_call(kernel, out_shape=[pltpu.VMEM(r.shape, r.dtype) for r in r...]
where the time goes in v2:
time: 57.5 us; the launch traced here: 57.3 us
  Pallas kernels  56.5 us (98%)
  between operations  0.81 us (1%)
    pallas_call x1, Pallas kernels, shards(): pl.pallas_call(kernel, out_shape=[pltpu.VMEM(r.shape, r.dtype) for r in r...  55.4 us

profile of v2, /device:TPU:1, one launch (start us, length us, event | category | flops | bytes accessed | tf_op | source)
XLA Modules:
  0.0 57.3 jit_solution(13612925562080962208)
XLA Ops:
  0.6 55.4 %step.1 = (bf16[512,1152]{1,0:T(8,128)(2,1)S(1)}, bf16[2,1152]{1,0:T(2,128)(2,1)S(1)}, f32[81,128]{1,0:T(8,128)S(1)}, f32[18,128]{1,0:T(8,128)S(1)}, f32[81,128]...) custom-call(bf16[512,1152]{1,0:T(8,128)(2,1)} %refs_0_.1, bf16[512,1152]{1,0:T(8,128)(2,1)} %refs_1_.1, ...), custom_call_target="tpu_custom_call" | custom-call | tf_op jit(solution)/shard_map/step/pallas_call | solution.py:538
  56.1 1.1 %write_out.1 = (bf16[512,1152]{1,0:T(8,128)(2,1)}, bf16[2,1152]{1,0:T(2,128)(2,1)}, f32[81,128]{1,0:T(8,128)}, f32[18,128]{1,0:T(8,128)}, f32[81,128]{1,0:T(8,12...) custom-call(bf16[512,1152]{1,0:T(8,128)(2,1)S(1)} %get-tuple-element.21.refs_0_, bf16[2,1152]{1,0:T(2,128)(2,1)S(1)} %get-tuple-element.22.refs_1_, ...), custom_call_target="tpu_custom_call" | custom-call | tf_op jit(solution)/shard_map/write_out/pallas_call | solution.py:549

commit v3 on v2

--- a/solution.py
+++ b/solution.py
@@ -25,9 +25,11 @@
 TILES = 9
 MINE = {0: (0, 5), 1: (5, 4)}
 UNITS = {
-    0: ((0, 0, 2), (1, 2, 2), (2, 4, 1)),
-    1: ((0, 0, 1), (1, 1, 1), (2, 2, 2)),
+    0: ((0, 0, 1), (1, 1, 1), (2, 2, 1), (0, 3, 1), (1, 4, 1)),
+    1: ((0, 0, 1), (1, 1, 1), (2, 2, 1), (2, 3, 1)),
 }
+E = 5
+FAR = [(a, b) for a in (2, 1, 3, 0) for b in (2, 1, 3, 0) if (a, b) != (0, 0)]
 EUNIT = {0: (2, 0, 5), 1: (0, 0, 4)}
 SLOTS = 5
 PHASES = False
@@ -94,13 +96,14 @@
     phase("start")
     loads = []
     for k, (src, dst) in enumerate((
-        (att_h, s.att), (cot_h, s.cot), (mp_h, s.st.at[core, 0]), (op_h, s.st.at[core, 1]),
-        (sp_h, s.st.at[core, 2]), (me_h, s.ste.at[core, 0]), (oe_h, s.ste.at[core, 1]),
-        (se_h, s.ste.at[core, 2]), (nxt_h, s.nxt), (tn_h, s.now), (tx_h, s.later), (ec_h, s.ecot),
+        (att_h, s.att), (cot_h, s.cot), (tn_h, s.now), (tx_h, s.later), (ec_h, s.ecot),
+        (mp_h, s.st.at[core, 0]), (op_h, s.st.at[core, 1]), (sp_h, s.st.at[core, 2]),
+        (me_h, s.ste.at[core, 0]), (oe_h, s.ste.at[core, 1]), (se_h, s.ste.at[core, 2]),
+        (nxt_h, s.nxt),
     )):
-        copy = pltpu.make_async_copy(src, dst, s.load_sem.at[k])
+        loads.append(pltpu.make_async_copy(src, dst, s.load_sem.at[k]))
+    for copy in loads[:5]:
         copy.start()
-        loads.append(copy)
 
     phase("signal")
     barrier = pltpu.get_barrier_semaphore()
@@ -117,81 +120,97 @@
     for spot in everyone:
         pl.semaphore_signal(barrier, inc=1, device_id=spot, device_id_type=MESH)
 
-    phase("freqs")
-    for k in (9, 10, 11):
-        loads[k].wait()
-    t_now, t_next, ecot = s.now, s.later, s.ecot
-    ladder = lax.broadcasted_iota(jnp.int32, (8, 128), 1).astype(F32)
-    line = lax.broadcasted_iota(jnp.int32, (8, 128), 0)
-    freqs = jnp.exp(-math.log(10000.0) * ladder / 128)
-    moments = jnp.where(
-        line == 0, t_now[0], jnp.where(line == 1, t_now[1], jnp.where(line == 2, t_next[0], t_next[1]))
-    )
-    phases = (moments * 1000.0) * freqs
-    waves = jnp.concatenate([jnp.cos(phases), jnp.sin(phases)], axis=1).astype(BF16)
-    columns = jnp.transpose(waves.astype(F32), (1, 0))
-
-    phase("transpose")
+    def paired(tiles):
+        return [tiles[k : k + 2] for k in range(0, len(tiles), 2)]
+
+    def terms(tiles):
+        t0, n = tiles[0], len(tiles)
+        both = lax.dot_general(
+            s.att[...], s.cot[:, t0 * 128 : (t0 + n) * 128], (((0,), (0,)), ((), ())),
+            preferred_element_type=F32,
+        )
+        return [both[:, k * 128 : k * 128 + 128] for k in range(n)]
+
+    phase("load")
     loads[0].wait()
-    s.attT[...] = jnp.transpose(s.att[...], (1, 0))
     loads[1].wait()
-
-    phase("eterms")
-    def term(t):
-        return jnp.dot(s.attT[...], s.cot[:, t * 128 : t * 128 + 128], preferred_element_type=F32)
-
-    cots = ecot[...].astype(F32)
-
-    def eterm(t):
-        c = cots[:, t * 128 : t * 128 + 128]
-        return columns[:, 0:1] * c[0:1] + columns[:, 1:2] * c[1:2]
-
-    for j in range(ocount):
-        s.psE[j] = eterm(ofirst + j).astype(BF16)
-    phase("barrier")
-    pl.semaphore_wait(barrier, len(everyone))
-    phase("partner_terms")
-    for k, src in enumerate((mp_h, op_h, sp_h)):
-        remote(src, s.st.at[core, k], s.dsend.at[k], s.drecv.at[k], partner)
-    for k, src in enumerate((me_h, oe_h, se_h)):
-        remote(src, s.ste.at[core, k], s.dsend.at[3 + k], s.drecv.at[3 + k], partner)
-    remote(s.psE.at[pl.ds(0, ocount)], s.prE.at[pl.ds(0, ocount)], s.dsend.at[6], s.drecv.at[6], partner)
-    for j in range(ocount):
-        s.ps[j] = term(ofirst + j).astype(BF16)
-        remote(s.ps.at[j], s.pr.at[j], s.psend.at[j], s.precv.at[j], partner)
-    phase("own_terms")
-    for j in range(count):
-        s.acc[j] = term(first + j)
+    for copy in loads[5:]:
+        copy.start()
+
+    for k, tiles in enumerate(paired(list(range(ofirst, ofirst + ocount)))):
+        phase(f"partner_terms{k}")
+        parts = terms(tiles)
+        for t, part in zip(tiles, parts):
+            s.ps[t - ofirst] = part.astype(BF16)
+        if k == 0:
+            phase("barrier")
+            pl.semaphore_wait(barrier, len(everyone))
+        for t in tiles:
+            remote(s.ps.at[t - ofirst], s.pr.at[t - ofirst], s.psend.at[t - ofirst], s.precv.at[t - ofirst], partner)
 
     x2 = s.x.reshape(SLOTS, 1152, 128)
     xe2 = s.xE.reshape(SLOTS, 256, 128)
 
     def stage_one(u, x, r1, q, j0, n):
-        for d in (1, 2, 3):
+        for d in (1, 3, 2):
             spot = at(q, d)
             remote(
                 x.at[(pl.ds(j0, n),) + cut(q, spot[q])],
                 r1.at[pl.ds(j0, n), d],
                 s.send1.at[u], s.recv1.at[u], spot,
             )
+
+    def keep_one(x, r1, q, j0, n):
         for j in range(j0, j0 + n):
             r1[j, 0] = x[(j,) + cut(q, pos[q])]
 
+    for tiles in paired(list(range(first, first + count))):
+        phase(f"own_terms{tiles[0] - first}")
+        parts = terms(tiles)
+        for t, part in zip(tiles, parts):
+            j = t - first
+            got(s.pr.at[j], s.precv.at[j])
+            x2[j] = (part + s.pr[j].astype(F32)).astype(BF16)
+            stage_one(j, s.x, s.r1, *units[j])
+
+    phase("freqs")
+    for k, src in enumerate((mp_h, op_h, sp_h)):
+        remote(src, s.st.at[core, k], s.dsend.at[k], s.drecv.at[k], partner)
+    for k, src in enumerate((me_h, oe_h, se_h)):
+        remote(src, s.ste.at[core, k], s.dsend.at[3 + k], s.drecv.at[3 + k], partner)
+    for k in (2, 3, 4):
+        loads[k].wait()
+    ladder = lax.broadcasted_iota(jnp.int32, (8, 128), 1).astype(F32)
+    line = lax.broadcasted_iota(jnp.int32, (8, 128), 0)
+    freqs = jnp.exp(-math.log(10000.0) * ladder / 128)
+    moments = jnp.where(
+        line == 0, s.now[0], jnp.where(line == 1, s.now[1], jnp.where(line == 2, s.later[0], s.later[1]))
+    )
+    phases = (moments * 1000.0) * freqs
+    waves = jnp.concatenate([jnp.cos(phases), jnp.sin(phases)], axis=1).astype(BF16)
+    columns = jnp.transpose(waves.astype(F32), (1, 0))
+    cots = s.ecot[...].astype(F32)
+
+    def eterm(t):
+        c = cots[:, t * 128 : t * 128 + 128]
+        return columns[:, 0:1] * c[0:1] + columns[:, 1:2] * c[1:2]
+
+    phase("eterms")
+    for j in range(ocount):
+        s.psE[j] = eterm(ofirst + j).astype(BF16)
+    remote(s.psE.at[pl.ds(0, ocount)], s.prE.at[pl.ds(0, ocount)], s.dsend.at[6], s.drecv.at[6], partner)
+    for unit in units:
+        keep_one(s.x, s.r1, *unit)
     phase("chip_e")
     got(s.prE.at[pl.ds(0, count)], s.drecv.at[6])
     for j in range(count):
         xe2[j] = (eterm(first + j) + s.prE[j].astype(F32)).astype(BF16)
-    stage_one(3, s.xE, s.r1E, *eunit)
-    for u, (q, j0, n) in enumerate(units):
-        phase(f"chip{u}")
-        for j in range(j0, j0 + n):
-            got(s.pr.at[j], s.precv.at[j])
-            x2[j] = (s.acc[j] + s.pr[j].astype(F32)).astype(BF16)
-        stage_one(u, s.x, s.r1, q, j0, n)
+    stage_one(E, s.xE, s.r1E, *eunit)
+    keep_one(s.xE, s.r1E, *eunit)
 
     phase("state")
     for k in range(6):
-        loads[2 + k].wait()
+        loads[5 + k].wait()
     for k in range(3):
         got(s.st.at[other, k], s.drecv.at[k])
         got(s.ste.at[other, k], s.drecv.at[3 + k])
@@ -214,50 +233,46 @@
             for d in (1, 2, 3):
                 total = total + r1v[j, d].astype(F32)
             y2[j] = total.astype(BF16)
-        for a in range(4):
-            for b in range(4):
-                if (a, b) == (0, 0):
-                    continue
-                spot = in_plane(q, a, b)
-                p1, p2 = plane_of(q, spot)
-                remote(
-                    y.at[pl.ds(j0, n), p1, p2],
-                    r2.at[pl.ds(j0, n), a * 4 + b, pl.ds(0, words)],
-                    s.send2.at[u], s.recv2.at[u], spot,
-                )
+        for a, b in FAR:
+            spot = in_plane(q, a, b)
+            p1, p2 = plane_of(q, spot)
+            remote(
+                y.at[pl.ds(j0, n), p1, p2],
+                r2.at[pl.ds(j0, n), a * 4 + b, pl.ds(0, words)],
+                s.send2.at[u], s.recv2.at[u], spot,
+            )
         p1, p2 = plane_of(q, pos)
         for j in range(j0, j0 + n):
             r2[j, 0, 0:words] = y[j, p1, p2]
 
-    phase("two_e")
-    stage_two(3, s.r1E, r1ve, s.yE, y2e, s.r2E, 2, *eunit)
     for u, unit in enumerate(units):
         phase(f"two{u}")
         stage_two(u, s.r1, r1v, s.y, y2, s.r2, 9, *unit)
+    phase("two_e")
+    stage_two(E, s.r1E, r1ve, s.yE, y2e, s.r2E, 2, *eunit)
 
     r2v = s.r2.reshape(SLOTS, 16, 24, 128)
     r2ve = s.r2E.reshape(SLOTS, 16, 8, 128)
     squares = jnp.zeros((24, 128), F32)
     squares_e = jnp.zeros((8, 128), F32)
-
+    for u, (q, j0, n) in enumerate(units):
+        phase(f"sum{u}")
+        got(s.r2.at[pl.ds(j0, n), pl.ds(1, 15), pl.ds(0, 9)], s.recv2.at[u])
+        for j in range(j0, j0 + n):
+            total = r2v[j, 0].astype(F32)
+            for k in range(1, 16):
+                total = total + r2v[j, k].astype(F32)
+            s.g[j] = total
+            squares = squares + total * total
     phase("sum_e")
     q, j0, n = eunit
-    got(s.r2E.at[pl.ds(j0, n), pl.ds(1, 15), pl.ds(0, 2)], s.recv2.at[3])
+    got(s.r2E.at[pl.ds(j0, n), pl.ds(1, 15), pl.ds(0, 2)], s.recv2.at[E])
     for j in range(j0, j0 + n):
         total = r2ve[j, 0].astype(F32)
         for k in range(1, 16):
             total = total + r2ve[j, k].astype(F32)
         s.gE[j] = total
         squares_e = squares_e + total * total
-    for u, (q, j0, n) in enumerate(units):
-        phase(f"sum{u}")
-        got(s.r2.at[pl.ds(j0, n), pl.ds(1, 15), pl.ds(0, 9)], s.recv2.at[u])
-        for j in range(j0, j0 + n):
-            total = r2v[j, 0].astype(F32)
-            for k in range(1, 16):
-                total = total + r2v[j, k].astype(F32)
-            s.g[j] = total
-            squares = squares + total * total
 
     phase("squares")
     rows = lax.broadcasted_iota(jnp.int32, (24, 128), 0)
@@ -270,17 +285,15 @@
     got(s.na.at[other], s.nrecv.at[0])
     pz, py, px = pos[:3]
     s.nb[pz, py] = s.na[0] + s.na[1]
-    for a in range(4):
-        for b in range(4):
-            if (a, b) != (0, 0):
-                remote(s.nb.at[pz, py], s.nb.at[pz, py], s.nsend.at[1], s.nrecv.at[1], in_plane(2, a, b))
+    for a, b in FAR:
+        remote(s.nb.at[pz, py], s.nb.at[pz, py], s.nsend.at[1], s.nrecv.at[1], in_plane(2, a, b))
     phase("norm_b")
     got(s.nw.at[pl.ds(0, 15)], s.nrecv.at[1])
     total = s.nb[0, 0]
     for k in range(1, 16):
         total = total + s.nb[k // 4, k % 4]
     s.nc[px] = total
-    for d in (1, 2, 3):
+    for d in (2, 1, 3):
         remote(s.nc.at[px], s.nc.at[px], s.nsend.at[2], s.nrecv.at[2], at(2, d))
     phase("norm_c")
     got(s.nw.at[pl.ds(0, 3)], s.nrecv.at[2])
@@ -299,22 +312,22 @@
             dirs[1, j] = fresh
             z2[j] = fresh.astype(BF16)
         p1, p2 = plane_of(q, pos)
-        for a in range(4):
-            for b in range(4):
-                if (a, b) == (0, 0):
-                    continue
-                remote(
-                    zz.at[pl.ds(j0, n), pl.ds(0, words)],
-                    v.at[pl.ds(j0, n), p1, p2],
-                    s.send3.at[u], s.recv3.at[u], in_plane(q, a, b),
-                )
+        for a, b in FAR:
+            remote(
+                zz.at[pl.ds(j0, n), pl.ds(0, words)],
+                v.at[pl.ds(j0, n), p1, p2],
+                s.send3.at[u], s.recv3.at[u], in_plane(q, a, b),
+            )
         for j in range(j0, j0 + n):
             v[j, p1, p2] = zz[j, 0:words]
 
+    order = [0, 1, 2, E] + list(range(3, count))
     phase("update")
-    for u, unit in enumerate(units):
-        update(u, s.g, s.reg, s.zz, z2, s.dirs, s.v, 9, *unit)
-    update(3, s.gE, s.regE, s.zE, z2e, s.dirsE, s.vE, 2, *eunit)
+    for u in order:
+        if u == E:
+            update(E, s.gE, s.regE, s.zE, z2e, s.dirsE, s.vE, 2, *eunit)
+        else:
+            update(u, s.g, s.reg, s.zz, z2, s.dirs, s.v, 9, *units[u])
 
     phase("outs")
     for k in range(2):
@@ -330,20 +343,19 @@
 
     def ring(u, r2, v, w, words, q, j0, n):
         got(r2.at[pl.ds(j0, n), pl.ds(1, 15), pl.ds(0, words)], s.recv3.at[u])
-        for d in (1, 2, 3):
-            remote(
-                v.at[pl.ds(j0, n)],
-                w.at[(pl.ds(first + j0, n),) + cut(q, pos[q])],
-                s.send4.at[u], s.recv4.at[u], at(q, d),
-            )
+        place = w.at[(pl.ds(first + j0, n),) + cut(q, pos[q])]
+        for d in (1, 3, 2):
+            remote(v.at[pl.ds(j0, n)], place, s.send4.at[u], s.recv4.at[u, d - 1], at(q, d))
+        remote(v.at[pl.ds(j0, n)], place, s.send5.at[u], s.recv5.at[u], partner)
         for j in range(j0, j0 + n):
             w[(first + j,) + cut(q, pos[q])] = v[j]
 
-    for u, unit in enumerate(units):
+    for u in order:
         phase(f"ring{u}")
-        ring(u, s.r2, s.v, s.w, 9, *unit)
-    phase("ring_e")
-    ring(3, s.r2E, s.vE, s.wE, 2, *eunit)
+        if u == E:
+            ring(E, s.r2E, s.vE, s.wE, 2, *eunit)
+        else:
+            ring(u, s.r2, s.v, s.w, 9, *units[u])
 
     phase("outs2")
     got(s.orr, s.drecv.at[7])
@@ -353,39 +365,53 @@
             out[pl.ds(ofirst + j, 9, stride=9), :] = s.orr[k, j, 0:9]
             oute[pl.ds(ofirst + j, 2, stride=9), :] = s.orrE[k, j, 0:2]
 
-    loads[8].wait()
+    loads[11].wait()
     w2 = s.w.reshape(TILES, 1152, 128)
     we2 = s.wE.reshape(TILES, 256, 128)
 
-    def product(t):
-        o_np[:, t * 128 : t * 128 + 128] = jnp.dot(
-            s.nxt[...], w2[t], preferred_element_type=F32
-        ).astype(BF16)
-
-    for u, (q, j0, n) in enumerate(units):
+    def own(u, v=s.v, w=s.w, unit=None):
         phase(f"own{u}")
-        got(s.r1.at[pl.ds(j0, n), pl.ds(1, 3)], s.recv4.at[u])
-        whole = s.w.at[pl.ds(first + j0, n)]
-        remote(whole, whole, s.send5.at[u], s.recv5.at[u], partner)
-        for j in range(j0, j0 + n):
-            product(first + j)
-    phase("own_e")
-    q, j0, n = eunit
-    got(s.r1E.at[pl.ds(j0, n), pl.ds(1, 3)], s.recv4.at[3])
-    whole = s.wE.at[pl.ds(first, count)]
-    remote(whole, whole, s.send5.at[3], s.recv5.at[3], partner)
-    for u, (q, j0, n) in enumerate(UNITS[other]):
+        q, j0, n = unit or units[u]
+        for d in (1, 3, 2):
+            got(v.at[pl.ds(j0, n)], s.recv4.at[u, d - 1])
+            quarter = w.at[(pl.ds(first + j0, n),) + cut(q, at(q, 4 - d)[q])]
+            remote(quarter, quarter, s.send5.at[u], s.recv5.at[u], partner)
+
+    def theirs(u):
         phase(f"theirs{u}")
-        got(s.w.at[pl.ds(ofirst + j0, n)], s.recv5.at[u])
-        for j in range(j0, j0 + n):
-            product(ofirst + j)
+        got(s.w.at[ofirst + u], s.recv5.at[u])
+
+    def product(*tiles):
+        phase(f"product{tiles[0]}")
+        whole = jnp.concatenate([w2[t] for t in tiles], axis=1)
+        mixed = jnp.dot(s.nxt[...], whole, preferred_element_type=F32).astype(BF16)
+        for k, t in enumerate(tiles):
+            o_np[:, t * 128 : t * 128 + 128] = mixed[:, k * 128 : k * 128 + 128]
+
+    for u in (0, 1, 2):
+        own(u)
+    product(first, first + 1)
+    theirs(0)
+    product(first + 2, ofirst)
+    own(E, s.vE, s.wE, eunit)
+    for u in range(3, count):
+        own(u)
+    theirs(1)
+    theirs(2)
+    product(ofirst + 1, ofirst + 2)
+    product(*range(first + 3, first + count))
     phase("last_e")
-    got(s.wE.at[pl.ds(ofirst, ocount)], s.recv5.at[3])
-    for t in range(TILES):
-        mixed = jnp.dot(waves, we2[t], preferred_element_type=F32)
-        o_ne[:, t * 128 : t * 128 + 128] = mixed[2:4].astype(BF16)
+    got(s.wE.at[pl.ds(ofirst, ocount)], s.recv5.at[E])
+    for t in range(0, TILES, 3):
+        whole = jnp.concatenate([we2[t], we2[t + 1], we2[t + 2]], axis=1)
+        mixed = jnp.dot(waves, whole, preferred_element_type=F32)
+        o_ne[:, t * 128 : t * 128 + 384] = mixed[2:4].astype(BF16)
+    for u in range(3, ocount):
+        theirs(u)
+    product(*range(ofirst + 3, ofirst + ocount))
 
     phase("drain")
+
     def sent(ref, sem):
         pltpu.make_async_remote_copy(
             src_ref=ref, dst_ref=ref, send_sem=sem, recv_sem=sem,
@@ -410,11 +436,11 @@
         sent(s.r1.at[pl.ds(j0, n), pl.ds(1, 3)], s.send4.at[u])
         sent(s.w.at[pl.ds(first + j0, n)], s.send5.at[u])
     q, j0, n = eunit
-    sent(s.r1E.at[pl.ds(j0, n), pl.ds(1, 3)], s.send1.at[3])
-    sent(s.r2E.at[pl.ds(j0, n), pl.ds(1, 15), pl.ds(0, 2)], s.send2.at[3])
-    sent(s.r2E.at[pl.ds(j0, n), pl.ds(1, 15), pl.ds(0, 2)], s.send3.at[3])
-    sent(s.r1E.at[pl.ds(j0, n), pl.ds(1, 3)], s.send4.at[3])
-    sent(s.wE.at[pl.ds(first, count)], s.send5.at[3])
+    sent(s.r1E.at[pl.ds(j0, n), pl.ds(1, 3)], s.send1.at[E])
+    sent(s.r2E.at[pl.ds(j0, n), pl.ds(1, 15), pl.ds(0, 2)], s.send2.at[E])
+    sent(s.r2E.at[pl.ds(j0, n), pl.ds(1, 15), pl.ds(0, 2)], s.send3.at[E])
+    sent(s.r1E.at[pl.ds(j0, n), pl.ds(1, 3)], s.send4.at[E])
+    sent(s.wE.at[pl.ds(first, count)], s.send5.at[E])
     phase(None)
 
 
@@ -443,14 +469,12 @@
     ecot=pltpu.VMEM((2, 1152), BF16),
     now=pltpu.SMEM((2,), F32),
     later=pltpu.SMEM((2,), F32),
-    attT=pltpu.VMEM((1152, 512), BF16),
     st=pltpu.VMEM((2, 3, 81, 128), F32),
     ste=pltpu.VMEM((2, 3, 18, 128), F32),
     ps=pltpu.VMEM((SLOTS, 1152, 128), BF16),
     pr=pltpu.VMEM((SLOTS, 1152, 128), BF16),
     psE=pltpu.VMEM((SLOTS, 256, 128), BF16),
     prE=pltpu.VMEM((SLOTS, 256, 128), BF16),
-    acc=pltpu.VMEM((SLOTS, 1152, 128), F32),
     x=pltpu.VMEM((SLOTS, 4, 4, 4, 9, 2, 128), BF16),
     xE=pltpu.VMEM((SLOTS, 4, 4, 4, 2, 2, 128), BF16),
     r1=pltpu.VMEM((SLOTS, 4, 4, 4, 9, 2, 128), BF16),
@@ -484,16 +508,16 @@
     drecv=DMA((9,)),
     psend=DMA((SLOTS,)),
     precv=DMA((SLOTS,)),
-    send1=DMA((4,)),
-    recv1=DMA((4,)),
-    send2=DMA((4,)),
-    recv2=DMA((4,)),
-    send3=DMA((4,)),
-    recv3=DMA((4,)),
-    send4=DMA((4,)),
-    recv4=DMA((4,)),
-    send5=DMA((4,)),
-    recv5=DMA((4,)),
+    send1=DMA((6,)),
+    recv1=DMA((6,)),
+    send2=DMA((6,)),
+    recv2=DMA((6,)),
+    send3=DMA((6,)),
+    recv3=DMA((6,)),
+    send4=DMA((6,)),
+    recv4=DMA((6, 3)),
+    send5=DMA((6,)),
+    recv5=DMA((6,)),
     nsend=DMA((3,)),
     nrecv=DMA((3,)),
 )

time: 57.5 us -> 54.2 us (0.943)
  Pallas kernels: 56.5 us -> 53.3 us
    pallas_call x1, Pallas kernels: 55.4 us -> 52.2 us  [shards(): pl.pallas_call(kernel, out_shape=[pltpu.VMEM(r.shape, r.dtype) for r in r...]
where the time goes in v3:
time: 54.2 us; the launch traced here: 54.1 us
  Pallas kernels  53.3 us (98%)
  between operations  0.81 us (1%)
    pallas_call x1, Pallas kernels, shards(): pl.pallas_call(kernel, out_shape=[pltpu.VMEM(r.shape, r.dtype) for r in r...  52.2 us
    pallas_call x1, Pallas kernels, shards(): pl.pallas_call(write_out, out_shape=results, in_specs=[vmem] * 7, out_spe...  1.1 us

profile of v3, /device:TPU:1, one launch (start us, length us, event | category | flops | bytes accessed | tf_op | source)
XLA Modules:
  0.0 54.1 jit_solution(7616089472191197258)
XLA Ops:
  0.6 52.2 %step.1 = (bf16[512,1152]{1,0:T(8,128)(2,1)S(1)}, bf16[2,1152]{1,0:T(2,128)(2,1)S(1)}, f32[81,128]{1,0:T(8,128)S(1)}, f32[18,128]{1,0:T(8,128)S(1)}, f32[81,128]...) custom-call(bf16[512,1152]{1,0:T(8,128)(2,1)} %refs_0_.1, bf16[512,1152]{1,0:T(8,128)(2,1)} %refs_1_.1, ...), custom_call_target="tpu_custom_call" | custom-call | tf_op jit(solution)/shard_map/step/pallas_call | solution.py:562
  52.8 1.1 %write_out.1 = (bf16[512,1152]{1,0:T(8,128)(2,1)}, bf16[2,1152]{1,0:T(2,128)(2,1)}, f32[81,128]{1,0:T(8,128)}, f32[18,128]{1,0:T(8,128)}, f32[81,128]{1,0:T(8,12...) custom-call(bf16[512,1152]{1,0:T(8,128)(2,1)S(1)} %get-tuple-element.21.refs_0_, bf16[2,1152]{1,0:T(2,128)(2,1)S(1)} %get-tuple-element.22.refs_1_, ...), custom_call_target="tpu_custom_call" | custom-call | tf_op jit(solution)/shard_map/write_out/pallas_call | solution.py:573

commit v4 on v3

--- a/solution.py
+++ b/solution.py
@@ -29,8 +29,11 @@
     1: ((0, 0, 1), (1, 1, 1), (2, 2, 1), (2, 3, 1)),
 }
 E = 5
+AROUND = [
+    (a, b, c) for a in (2, 1, 3, 0) for b in (2, 1, 3, 0) for c in (2, 1, 3, 0) if (a, b, c) != (0, 0, 0)
+]
 FAR = [(a, b) for a in (2, 1, 3, 0) for b in (2, 1, 3, 0) if (a, b) != (0, 0)]
-EUNIT = {0: (2, 0, 5), 1: (0, 0, 4)}
+EUNIT = {0: (1, 0, 5), 1: (0, 0, 4)}
 SLOTS = 5
 PHASES = False
 
@@ -92,31 +95,32 @@
             device_id=partner, device_id_type=MESH,
         ).wait_recv()
 
+    def sent(ref, sem):
+        pltpu.make_async_remote_copy(
+            src_ref=ref, dst_ref=ref, send_sem=sem, recv_sem=sem,
+            device_id=partner, device_id_type=MESH,
+        ).wait_send()
+
     phase = Phase()
     phase("start")
-    loads = []
-    for k, (src, dst) in enumerate((
-        (att_h, s.att), (cot_h, s.cot), (tn_h, s.now), (tx_h, s.later), (ec_h, s.ecot),
-        (mp_h, s.st.at[core, 0]), (op_h, s.st.at[core, 1]), (sp_h, s.st.at[core, 2]),
-        (me_h, s.ste.at[core, 0]), (oe_h, s.ste.at[core, 1]), (se_h, s.ste.at[core, 2]),
-        (nxt_h, s.nxt),
-    )):
-        loads.append(pltpu.make_async_copy(src, dst, s.load_sem.at[k]))
-    for copy in loads[:5]:
-        copy.start()
+    def load(src, dst, k):
+        pltpu.make_async_copy(src, dst, s.load_sem.at[k]).start()
+
+    def loaded(ref, k):
+        pltpu.make_async_copy(ref, ref, s.load_sem.at[k]).wait()
+
+    load(tn_h, s.now, 0)
+    load(tx_h, s.later, 1)
+    load(ec_h, s.ecot, 2)
+    load(att_h, s.att, 3)
+    load(cot_h, s.cot, 4)
 
     phase("signal")
     barrier = pltpu.get_barrier_semaphore()
-    peers = {}
-    for q in range(3):
-        for a in range(4):
-            for b in range(4):
-                if (a, b) != (0, 0):
-                    key = [0, 0, 0]
-                    i, j = [k for k in range(3) if k != q]
-                    key[i], key[j] = a, b
-                    peers[tuple(key)] = in_plane(q, a, b)
-    everyone = [tuple(p) for _, p in sorted(peers.items())] + [partner]
+    around = [
+        tuple(lax.rem(pos[k] + d[k], 4) for k in range(3)) + (pos[3],) for d in AROUND
+    ]
+    everyone = around + [partner]
     for spot in everyone:
         pl.semaphore_signal(barrier, inc=1, device_id=spot, device_id_type=MESH)
 
@@ -124,62 +128,16 @@
         return [tiles[k : k + 2] for k in range(0, len(tiles), 2)]
 
     def terms(tiles):
-        t0, n = tiles[0], len(tiles)
-        both = lax.dot_general(
-            s.att[...], s.cot[:, t0 * 128 : (t0 + n) * 128], (((0,), (0,)), ((), ())),
-            preferred_element_type=F32,
-        )
-        return [both[:, k * 128 : k * 128 + 128] for k in range(n)]
-
-    phase("load")
-    loads[0].wait()
-    loads[1].wait()
-    for copy in loads[5:]:
-        copy.start()
-
-    for k, tiles in enumerate(paired(list(range(ofirst, ofirst + ocount)))):
-        phase(f"partner_terms{k}")
-        parts = terms(tiles)
-        for t, part in zip(tiles, parts):
-            s.ps[t - ofirst] = part.astype(BF16)
-        if k == 0:
-            phase("barrier")
-            pl.semaphore_wait(barrier, len(everyone))
-        for t in tiles:
-            remote(s.ps.at[t - ofirst], s.pr.at[t - ofirst], s.psend.at[t - ofirst], s.precv.at[t - ofirst], partner)
-
-    x2 = s.x.reshape(SLOTS, 1152, 128)
-    xe2 = s.xE.reshape(SLOTS, 256, 128)
-
-    def stage_one(u, x, r1, q, j0, n):
-        for d in (1, 3, 2):
-            spot = at(q, d)
-            remote(
-                x.at[(pl.ds(j0, n),) + cut(q, spot[q])],
-                r1.at[pl.ds(j0, n), d],
-                s.send1.at[u], s.recv1.at[u], spot,
-            )
-
-    def keep_one(x, r1, q, j0, n):
-        for j in range(j0, j0 + n):
-            r1[j, 0] = x[(j,) + cut(q, pos[q])]
-
-    for tiles in paired(list(range(first, first + count))):
-        phase(f"own_terms{tiles[0] - first}")
-        parts = terms(tiles)
-        for t, part in zip(tiles, parts):
-            j = t - first
-            got(s.pr.at[j], s.precv.at[j])
-            x2[j] = (part + s.pr[j].astype(F32)).astype(BF16)
-            stage_one(j, s.x, s.r1, *units[j])
+        cols = s.cot[:, tiles[0] * 128 : (tiles[-1] + 1) * 128]
+        return [
+            jnp.dot(s.attT[h * 576 : h * 576 + 576, :], cols, preferred_element_type=F32)
+            for h in range(2)
+        ]
 
     phase("freqs")
-    for k, src in enumerate((mp_h, op_h, sp_h)):
-        remote(src, s.st.at[core, k], s.dsend.at[k], s.drecv.at[k], partner)
-    for k, src in enumerate((me_h, oe_h, se_h)):
-        remote(src, s.ste.at[core, k], s.dsend.at[3 + k], s.drecv.at[3 + k], partner)
-    for k in (2, 3, 4):
-        loads[k].wait()
+    loaded(s.now, 0)
+    loaded(s.later, 1)
+    loaded(s.ecot, 2)
     ladder = lax.broadcasted_iota(jnp.int32, (8, 128), 1).astype(F32)
     line = lax.broadcasted_iota(jnp.int32, (8, 128), 0)
     freqs = jnp.exp(-math.log(10000.0) * ladder / 128)
@@ -195,25 +153,79 @@
         c = cots[:, t * 128 : t * 128 + 128]
         return columns[:, 0:1] * c[0:1] + columns[:, 1:2] * c[1:2]
 
-    phase("eterms")
     for j in range(ocount):
         s.psE[j] = eterm(ofirst + j).astype(BF16)
-    remote(s.psE.at[pl.ds(0, ocount)], s.prE.at[pl.ds(0, ocount)], s.dsend.at[6], s.drecv.at[6], partner)
-    for unit in units:
-        keep_one(s.x, s.r1, *unit)
+
+    phase("load")
+    loaded(s.att, 3)
+    s.attT[...] = jnp.transpose(s.att[...], (1, 0))
+    loaded(s.cot, 4)
+    for k, src in enumerate((mp_h, op_h, sp_h)):
+        load(src, s.st.at[core, k], 5)
+    for k, src in enumerate((me_h, oe_h, se_h)):
+        load(src, s.ste.at[core, k], 6)
+    load(nxt_h, s.nxt, 7)
+
+    for k, tiles in enumerate(paired(list(range(ofirst, ofirst + ocount)))):
+        phase(f"partner_terms{k}")
+        parts = terms(tiles)
+        for i, t in enumerate(tiles):
+            for h in range(2):
+                s.ps[t - ofirst, h * 576 : h * 576 + 576] = parts[h][:, i * 128 : i * 128 + 128].astype(BF16)
+        if k == 0:
+            phase("barrier")
+            pl.semaphore_wait(barrier, len(everyone))
+            remote(s.psE.at[pl.ds(0, ocount)], s.prE.at[pl.ds(0, ocount)], s.dsend.at[2], s.drecv.at[2], partner)
+        for t in tiles:
+            remote(s.ps.at[t - ofirst], s.pr.at[t - ofirst], s.psend, s.recvc.at[t - ofirst], partner)
+    for k, src in enumerate((mp_h, op_h, sp_h)):
+        remote(src, s.st.at[core, k], s.dsend.at[0], s.drecv.at[0], partner)
+    for k, src in enumerate((me_h, oe_h, se_h)):
+        remote(src, s.ste.at[core, k], s.dsend.at[1], s.drecv.at[1], partner)
+
+    x2 = s.x.reshape(SLOTS, 1152, 128)
+    xe2 = s.xE.reshape(SLOTS, 256, 128)
+
+    def stage_one(u, x, r1, q, j0, n):
+        for d in (1, 3, 2):
+            spot = at(q, d)
+            remote(
+                x.at[(pl.ds(j0, n),) + cut(q, spot[q])],
+                r1.at[pl.ds(j0, n), d],
+                s.senda.at[int(u == E)], s.recva.at[u], spot,
+            )
+
+    def keep_one(x, r1, q, j0, n):
+        for j in range(j0, j0 + n):
+            r1[j, 0] = x[(j,) + cut(q, pos[q])]
+
     phase("chip_e")
-    got(s.prE.at[pl.ds(0, count)], s.drecv.at[6])
+    got(s.prE.at[pl.ds(0, count)], s.drecv.at[2])
     for j in range(count):
         xe2[j] = (eterm(first + j) + s.prE[j].astype(F32)).astype(BF16)
     stage_one(E, s.xE, s.r1E, *eunit)
+
+    for tiles in paired(list(range(first, first + count))):
+        phase(f"own_terms{tiles[0] - first}")
+        parts = terms(tiles)
+        for i, t in enumerate(tiles):
+            j = t - first
+            got(s.pr.at[j], s.recvc.at[j])
+            for h in range(2):
+                part = parts[h][:, i * 128 : i * 128 + 128]
+                x2[j, h * 576 : h * 576 + 576] = (part + s.pr[j, h * 576 : h * 576 + 576].astype(F32)).astype(BF16)
+            stage_one(j, s.x, s.r1, *units[j])
+
+    phase("keep")
     keep_one(s.xE, s.r1E, *eunit)
+    for unit in units:
+        keep_one(s.x, s.r1, *unit)
 
     phase("state")
-    for k in range(6):
-        loads[5 + k].wait()
-    for k in range(3):
-        got(s.st.at[other, k], s.drecv.at[k])
-        got(s.ste.at[other, k], s.drecv.at[3 + k])
+    loaded(s.st.at[core], 5)
+    loaded(s.ste.at[core], 6)
+    got(s.st.at[other], s.drecv.at[0])
+    got(s.ste.at[other], s.drecv.at[1])
     for k in range(3):
         for j in range(count):
             t = first + j
@@ -227,7 +239,7 @@
     y2e = s.yE.reshape(SLOTS, 64, 128)
 
     def stage_two(u, r1, r1v, y, y2, r2, words, q, j0, n):
-        got(r1.at[pl.ds(j0, n), pl.ds(1, 3)], s.recv1.at[u])
+        got(r1.at[pl.ds(j0, n), pl.ds(1, 3)], s.recva.at[u])
         for j in range(j0, j0 + n):
             total = r1v[j, 0].astype(F32)
             for d in (1, 2, 3):
@@ -239,7 +251,7 @@
             remote(
                 y.at[pl.ds(j0, n), p1, p2],
                 r2.at[pl.ds(j0, n), a * 4 + b, pl.ds(0, words)],
-                s.send2.at[u], s.recv2.at[u], spot,
+                s.sendb.at[int(u == E)], s.recvb.at[u], spot,
             )
         p1, p2 = plane_of(q, pos)
         for j in range(j0, j0 + n):
@@ -257,7 +269,7 @@
     squares_e = jnp.zeros((8, 128), F32)
     for u, (q, j0, n) in enumerate(units):
         phase(f"sum{u}")
-        got(s.r2.at[pl.ds(j0, n), pl.ds(1, 15), pl.ds(0, 9)], s.recv2.at[u])
+        got(s.r2.at[pl.ds(j0, n), pl.ds(1, 15), pl.ds(0, 9)], s.recvb.at[u])
         for j in range(j0, j0 + n):
             total = r2v[j, 0].astype(F32)
             for k in range(1, 16):
@@ -266,7 +278,7 @@
             squares = squares + total * total
     phase("sum_e")
     q, j0, n = eunit
-    got(s.r2E.at[pl.ds(j0, n), pl.ds(1, 15), pl.ds(0, 2)], s.recv2.at[E])
+    got(s.r2E.at[pl.ds(j0, n), pl.ds(1, 15), pl.ds(0, 2)], s.recvb.at[E])
     for j in range(j0, j0 + n):
         total = r2ve[j, 0].astype(F32)
         for k in range(1, 16):
@@ -284,20 +296,21 @@
     phase("norm_a")
     got(s.na.at[other], s.nrecv.at[0])
     pz, py, px = pos[:3]
-    s.nb[pz, py] = s.na[0] + s.na[1]
-    for a, b in FAR:
-        remote(s.nb.at[pz, py], s.nb.at[pz, py], s.nsend.at[1], s.nrecv.at[1], in_plane(2, a, b))
+    mine = s.nb.at[pz, py, px]
+    s.nb[pz, py, px] = s.na[0] + s.na[1]
+    for spot in around:
+        remote(mine, mine, s.nsend.at[1], s.nrecv.at[1], spot)
+    sent(s.st.at[core], s.dsend.at[0])
+    sent(s.ste.at[core], s.dsend.at[1])
+    sent(s.r1.at[pl.ds(0, count), pl.ds(1, 3)], s.senda.at[0])
+    sent(s.r1E.at[pl.ds(0, count), pl.ds(1, 3)], s.senda.at[1])
+    sent(s.r2.at[pl.ds(0, count), pl.ds(1, 15), pl.ds(0, 9)], s.sendb.at[0])
+    sent(s.r2E.at[pl.ds(0, count), pl.ds(1, 15), pl.ds(0, 2)], s.sendb.at[1])
     phase("norm_b")
-    got(s.nw.at[pl.ds(0, 15)], s.nrecv.at[1])
-    total = s.nb[0, 0]
-    for k in range(1, 16):
-        total = total + s.nb[k // 4, k % 4]
-    s.nc[px] = total
-    for d in (2, 1, 3):
-        remote(s.nc.at[px], s.nc.at[px], s.nsend.at[2], s.nrecv.at[2], at(2, d))
-    phase("norm_c")
-    got(s.nw.at[pl.ds(0, 3)], s.nrecv.at[2])
-    total = s.nc[0] + s.nc[1] + s.nc[2] + s.nc[3]
+    got(s.nw, s.nrecv.at[1])
+    total = s.nb[0, 0, 0]
+    for k in range(1, 64):
+        total = total + s.nb[k // 16, k // 4 % 4, k % 4]
     grad_norm = jnp.sqrt(jnp.sum(total, axis=1, keepdims=True))
     clip = jnp.minimum(jnp.float32(1.0), max_norm / (grad_norm + 1e-06))
     o_norm[...] = jnp.broadcast_to(grad_norm, (1, 128))
@@ -316,12 +329,12 @@
             remote(
                 zz.at[pl.ds(j0, n), pl.ds(0, words)],
                 v.at[pl.ds(j0, n), p1, p2],
-                s.send3.at[u], s.recv3.at[u], in_plane(q, a, b),
+                s.senda.at[int(u == E)], s.recva.at[u], in_plane(q, a, b),
             )
         for j in range(j0, j0 + n):
             v[j, p1, p2] = zz[j, 0:words]
 
-    order = [0, 1, 2, E] + list(range(3, count))
+    order = list(range(count)) + [E]
     phase("update")
     for u in order:
         if u == E:
@@ -334,19 +347,19 @@
         for j in range(count):
             s.os[k, j, 0:9] = s.dirs[k, j, 9 * other : 9 * other + 9]
             s.osE[k, j, 0:2] = s.dirsE[k, j, 2 * other : 2 * other + 2]
-    remote(s.os, s.orr, s.dsend.at[7], s.drecv.at[7], partner)
-    remote(s.osE, s.orrE, s.dsend.at[8], s.drecv.at[8], partner)
+    remote(s.os, s.orr, s.dsend.at[0], s.drecv.at[0], partner)
+    remote(s.osE, s.orrE, s.dsend.at[1], s.drecv.at[1], partner)
     for k, (out, oute) in enumerate(((o_dir, o_dire), (o_mst, o_mste))):
         for j in range(count):
             out[pl.ds(first + j, 9, stride=9), :] = s.dirs[k, j, 9 * core : 9 * core + 9]
             oute[pl.ds(first + j, 2, stride=9), :] = s.dirsE[k, j, 2 * core : 2 * core + 2]
 
     def ring(u, r2, v, w, words, q, j0, n):
-        got(r2.at[pl.ds(j0, n), pl.ds(1, 15), pl.ds(0, words)], s.recv3.at[u])
+        got(r2.at[pl.ds(j0, n), pl.ds(1, 15), pl.ds(0, words)], s.recva.at[u])
         place = w.at[(pl.ds(first + j0, n),) + cut(q, pos[q])]
         for d in (1, 3, 2):
-            remote(v.at[pl.ds(j0, n)], place, s.send4.at[u], s.recv4.at[u, d - 1], at(q, d))
-        remote(v.at[pl.ds(j0, n)], place, s.send5.at[u], s.recv5.at[u], partner)
+            remote(v.at[pl.ds(j0, n)], place, s.sendb.at[int(u == E)], s.recvb.at[u], at(q, d))
+        remote(v.at[pl.ds(j0, n)], place, s.sendc.at[int(u == E)], s.recvc.at[u], partner)
         for j in range(j0, j0 + n):
             w[(first + j,) + cut(q, pos[q])] = v[j]
 
@@ -358,89 +371,66 @@
             ring(u, s.r2, s.v, s.w, 9, *units[u])
 
     phase("outs2")
-    got(s.orr, s.drecv.at[7])
-    got(s.orrE, s.drecv.at[8])
+    got(s.orr, s.drecv.at[0])
+    got(s.orrE, s.drecv.at[1])
     for k, (out, oute) in enumerate(((o_dir, o_dire), (o_mst, o_mste))):
         for j in range(ocount):
             out[pl.ds(ofirst + j, 9, stride=9), :] = s.orr[k, j, 0:9]
             oute[pl.ds(ofirst + j, 2, stride=9), :] = s.orrE[k, j, 0:2]
 
-    loads[11].wait()
+    loaded(s.nxt, 7)
     w2 = s.w.reshape(TILES, 1152, 128)
     we2 = s.wE.reshape(TILES, 256, 128)
 
-    def own(u, v=s.v, w=s.w, unit=None):
+    def own(u, r1, w, q, j0, n):
         phase(f"own{u}")
-        q, j0, n = unit or units[u]
+        got(r1.at[pl.ds(j0, n), pl.ds(1, 3)], s.recvb.at[u])
         for d in (1, 3, 2):
-            got(v.at[pl.ds(j0, n)], s.recv4.at[u, d - 1])
-            quarter = w.at[(pl.ds(first + j0, n),) + cut(q, at(q, 4 - d)[q])]
-            remote(quarter, quarter, s.send5.at[u], s.recv5.at[u], partner)
+            quarter = w.at[(pl.ds(first + j0, n),) + cut(q, at(q, d)[q])]
+            remote(quarter, quarter, s.sendc.at[int(u == E)], s.recvc.at[u], partner)
 
     def theirs(u):
         phase(f"theirs{u}")
-        got(s.w.at[ofirst + u], s.recv5.at[u])
-
-    def product(*tiles):
-        phase(f"product{tiles[0]}")
-        whole = jnp.concatenate([w2[t] for t in tiles], axis=1)
-        mixed = jnp.dot(s.nxt[...], whole, preferred_element_type=F32).astype(BF16)
-        for k, t in enumerate(tiles):
-            o_np[:, t * 128 : t * 128 + 128] = mixed[:, k * 128 : k * 128 + 128]
-
-    for u in (0, 1, 2):
-        own(u)
-    product(first, first + 1)
-    theirs(0)
-    product(first + 2, ofirst)
-    own(E, s.vE, s.wE, eunit)
-    for u in range(3, count):
-        own(u)
-    theirs(1)
-    theirs(2)
-    product(ofirst + 1, ofirst + 2)
-    product(*range(first + 3, first + count))
-    phase("last_e")
-    got(s.wE.at[pl.ds(ofirst, ocount)], s.recv5.at[E])
-    for t in range(0, TILES, 3):
-        whole = jnp.concatenate([we2[t], we2[t + 1], we2[t + 2]], axis=1)
+        got(s.w.at[ofirst + u], s.recvc.at[u])
+
+    def product(lo, hi):
+        phase(f"product{lo}")
+        whole = jnp.concatenate([w2[t] for t in range(lo, hi)], axis=1)
+        for h in range(2):
+            o_np[h * 256 : h * 256 + 256, lo * 128 : hi * 128] = jnp.dot(
+                s.nxt[h * 256 : h * 256 + 256, :], whole, preferred_element_type=F32
+            ).astype(BF16)
+
+    def eproduct(lo, hi):
+        phase(f"eproduct{lo}")
+        whole = jnp.concatenate([we2[t] for t in range(lo, hi)], axis=1)
         mixed = jnp.dot(waves, whole, preferred_element_type=F32)
-        o_ne[:, t * 128 : t * 128 + 384] = mixed[2:4].astype(BF16)
-    for u in range(3, ocount):
+        o_ne[:, lo * 128 : hi * 128] = mixed[2:4].astype(BF16)
+
+    for u in range(count):
+        own(u, s.r1, s.w, *units[u])
+    own(E, s.r1E, s.wE, *eunit)
+    product(first, first + count)
+    eproduct(first, first + count)
+    for u in range(ocount):
         theirs(u)
-    product(*range(ofirst + 3, ofirst + ocount))
+    got(s.wE.at[pl.ds(ofirst, ocount)], s.recvc.at[E])
+    product(ofirst, ofirst + ocount)
+    eproduct(ofirst, ofirst + ocount)
 
     phase("drain")
-
-    def sent(ref, sem):
-        pltpu.make_async_remote_copy(
-            src_ref=ref, dst_ref=ref, send_sem=sem, recv_sem=sem,
-            device_id=partner, device_id_type=MESH,
-        ).wait_send()
-
-    for k in range(3):
-        sent(s.st.at[core, k], s.dsend.at[k])
-        sent(s.ste.at[core, k], s.dsend.at[3 + k])
-    sent(s.psE.at[pl.ds(0, ocount)], s.dsend.at[6])
-    sent(s.os, s.dsend.at[7])
-    sent(s.osE, s.dsend.at[8])
-    for j in range(ocount):
-        sent(s.ps.at[j], s.psend.at[j])
+    sent(s.psE.at[pl.ds(0, ocount)], s.dsend.at[2])
+    sent(s.os, s.dsend.at[0])
+    sent(s.osE, s.dsend.at[1])
+    sent(s.ps.at[pl.ds(0, ocount)], s.psend)
     sent(s.na.at[core], s.nsend.at[0])
-    sent(s.nw.at[pl.ds(0, 15)], s.nsend.at[1])
-    sent(s.nw.at[pl.ds(0, 3)], s.nsend.at[2])
-    for u, (q, j0, n) in enumerate(units):
-        sent(s.r1.at[pl.ds(j0, n), pl.ds(1, 3)], s.send1.at[u])
-        sent(s.r2.at[pl.ds(j0, n), pl.ds(1, 15), pl.ds(0, 9)], s.send2.at[u])
-        sent(s.r2.at[pl.ds(j0, n), pl.ds(1, 15), pl.ds(0, 9)], s.send3.at[u])
-        sent(s.r1.at[pl.ds(j0, n), pl.ds(1, 3)], s.send4.at[u])
-        sent(s.w.at[pl.ds(first + j0, n)], s.send5.at[u])
-    q, j0, n = eunit
-    sent(s.r1E.at[pl.ds(j0, n), pl.ds(1, 3)], s.send1.at[E])
-    sent(s.r2E.at[pl.ds(j0, n), pl.ds(1, 15), pl.ds(0, 2)], s.send2.at[E])
-    sent(s.r2E.at[pl.ds(j0, n), pl.ds(1, 15), pl.ds(0, 2)], s.send3.at[E])
-    sent(s.r1E.at[pl.ds(j0, n), pl.ds(1, 3)], s.send4.at[E])
-    sent(s.wE.at[pl.ds(first, count)], s.send5.at[E])
+    sent(s.nw, s.nsend.at[1])
+    sent(s.r2.at[pl.ds(0, count), pl.ds(1, 15), pl.ds(0, 9)], s.senda.at[0])
+    sent(s.r2E.at[pl.ds(0, count), pl.ds(1, 15), pl.ds(0, 2)], s.senda.at[1])
+    sent(s.r1.at[pl.ds(0, count), pl.ds(1, 3)], s.sendb.at[0])
+    sent(s.r1E.at[pl.ds(0, count), pl.ds(1, 3)], s.sendb.at[1])
+    sent(s.w.at[pl.ds(first, count)], s.sendc.at[0])
+    sent(s.wE.at[pl.ds(first, count)], s.sendc.at[1])
     phase(None)
 
 
@@ -464,6 +454,7 @@
 DMA = pltpu.SemaphoreType.DMA
 SCRATCH = dict(
     att=pltpu.VMEM((512, 1152), BF16),
+    attT=pltpu.VMEM((1152, 512), BF16),
     cot=pltpu.VMEM((512, 1152), BF16),
     nxt=pltpu.VMEM((512, 1152), BF16),
     ecot=pltpu.VMEM((2, 1152), BF16),
@@ -500,26 +491,20 @@
     orr=pltpu.VMEM((2, SLOTS, 16, 128), F32),
     orrE=pltpu.VMEM((2, SLOTS, 8, 128), F32),
     na=pltpu.VMEM((2, 1, 128), F32),
-    nb=pltpu.VMEM((4, 4, 1, 128), F32),
-    nc=pltpu.VMEM((4, 1, 128), F32),
-    nw=pltpu.VMEM((15, 1, 128), F32),
-    load_sem=DMA((12,)),
-    dsend=DMA((9,)),
-    drecv=DMA((9,)),
-    psend=DMA((SLOTS,)),
-    precv=DMA((SLOTS,)),
-    send1=DMA((6,)),
-    recv1=DMA((6,)),
-    send2=DMA((6,)),
-    recv2=DMA((6,)),
-    send3=DMA((6,)),
-    recv3=DMA((6,)),
-    send4=DMA((6,)),
-    recv4=DMA((6, 3)),
-    send5=DMA((6,)),
-    recv5=DMA((6,)),
-    nsend=DMA((3,)),
-    nrecv=DMA((3,)),
+    nb=pltpu.VMEM((4, 4, 4, 1, 128), F32),
+    nw=pltpu.VMEM((63, 1, 128), F32),
+    load_sem=DMA((8,)),
+    dsend=DMA((3,)),
+    drecv=DMA((3,)),
+    psend=DMA(()),
+    senda=DMA((2,)),
+    sendb=DMA((2,)),
+    sendc=DMA((2,)),
+    recva=DMA((6,)),
+    recvb=DMA((6,)),
+    recvc=DMA((6,)),
+    nsend=DMA((2,)),
+    nrecv=DMA((2,)),
 )
 
 

time: 54.2 us -> 51.4 us (0.948)
  Pallas kernels: 53.3 us -> 50.5 us
    pallas_call x1, Pallas kernels: 52.2 us -> 49.4 us  [shards(): pl.pallas_call(kernel, out_shape=[pltpu.VMEM(r.shape, r.dtype) for r in r...]
where the time goes in v4:
time: 51.4 us; the launch traced here: 51.3 us
  Pallas kernels  50.5 us (98%)
  between operations  0.81 us (2%)
    pallas_call x1, Pallas kernels, shards(): pl.pallas_call(kernel, out_shape=[pltpu.VMEM(r.shape, r.dtype) for r in r...  49.4 us
    pallas_call x1, Pallas kernels, shards(): pl.pallas_call(write_out, out_shape=results, in_specs=[vmem] * 7, out_spe...  1.1 us

profile of v4, /device:TPU:1, one launch (start us, length us, event | category | flops | bytes accessed | tf_op | source)
XLA Modules:
  0.0 51.3 jit_solution(1463333435157960336)
XLA Ops:
  0.6 49.4 %step.1 = (bf16[512,1152]{1,0:T(8,128)(2,1)S(1)}, bf16[2,1152]{1,0:T(2,128)(2,1)S(1)}, f32[81,128]{1,0:T(8,128)S(1)}, f32[18,128]{1,0:T(8,128)S(1)}, f32[81,128]...) custom-call(bf16[512,1152]{1,0:T(8,128)(2,1)} %refs_0_.1, bf16[512,1152]{1,0:T(8,128)(2,1)} %refs_1_.1, ...), custom_call_target="tpu_custom_call" | custom-call | tf_op jit(solution)/shard_map/step/pallas_call | solution.py:547
  50.0 1.1 %write_out.1 = (bf16[512,1152]{1,0:T(8,128)(2,1)}, bf16[2,1152]{1,0:T(2,128)(2,1)}, f32[81,128]{1,0:T(8,128)}, f32[18,128]{1,0:T(8,128)}, f32[81,128]{1,0:T(8,12...) custom-call(bf16[512,1152]{1,0:T(8,128)(2,1)S(1)} %get-tuple-element.21.refs_0_, bf16[2,1152]{1,0:T(2,128)(2,1)S(1)} %get-tuple-element.22.refs_1_, ...), custom_call_target="tpu_custom_call" | custom-call | tf_op jit(solution)/shard_map/write_out/pallas_call | solution.py:558

commit v5 on v4

--- a/solution.py
+++ b/solution.py
@@ -33,7 +33,7 @@
     (a, b, c) for a in (2, 1, 3, 0) for b in (2, 1, 3, 0) for c in (2, 1, 3, 0) if (a, b, c) != (0, 0, 0)
 ]
 FAR = [(a, b) for a in (2, 1, 3, 0) for b in (2, 1, 3, 0) if (a, b) != (0, 0)]
-EUNIT = {0: (1, 0, 5), 1: (0, 0, 4)}
+EUNIT = {0: (0, 0, 5), 1: (0, 0, 4)}
 SLOTS = 5
 PHASES = False
 
@@ -120,7 +120,8 @@
     around = [
         tuple(lax.rem(pos[k] + d[k], 4) for k in range(3)) + (pos[3],) for d in AROUND
     ]
-    everyone = around + [partner]
+    beside = [tuple(at(0, d)[:3]) + (c,) for d in range(4) for c in (core, other)][1:]
+    everyone = around + [spot for spot in beside if spot[3] == other]
     for spot in everyone:
         pl.semaphore_signal(barrier, inc=1, device_id=spot, device_id_type=MESH)
 
@@ -145,16 +146,14 @@
         line == 0, s.now[0], jnp.where(line == 1, s.now[1], jnp.where(line == 2, s.later[0], s.later[1]))
     )
     phases = (moments * 1000.0) * freqs
-    waves = jnp.concatenate([jnp.cos(phases), jnp.sin(phases)], axis=1).astype(BF16)
-    columns = jnp.transpose(waves.astype(F32), (1, 0))
-    cots = s.ecot[...].astype(F32)
-
-    def eterm(t):
-        c = cots[:, t * 128 : t * 128 + 128]
-        return columns[:, 0:1] * c[0:1] + columns[:, 1:2] * c[1:2]
-
-    for j in range(ocount):
-        s.psE[j] = eterm(ofirst + j).astype(BF16)
+    waves = [jnp.cos(phases), jnp.sin(phases)]
+    slot = pos[0] * 2 + core
+    for k in range(TILES):
+        s.eb[k, slot] = s.ecot[:, k * 128 : k * 128 + 128]
+    for k in range(2):
+        s.eb[TILES + k, slot] = waves[k][0:2].astype(BF16)
+        s.eb[TILES + 2 + k, slot] = waves[k][2:4].astype(BF16)
+    s.wz[...] = jnp.zeros(s.wz.shape, BF16)
 
     phase("load")
     loaded(s.att, 3)
@@ -175,7 +174,8 @@
         if k == 0:
             phase("barrier")
             pl.semaphore_wait(barrier, len(everyone))
-            remote(s.psE.at[pl.ds(0, ocount)], s.prE.at[pl.ds(0, ocount)], s.dsend.at[2], s.drecv.at[2], partner)
+            for spot in beside:
+                remote(s.eb.at[:, slot], s.eb.at[:, slot], s.dsend.at[2], s.drecv.at[2], spot)
         for t in tiles:
             remote(s.ps.at[t - ofirst], s.pr.at[t - ofirst], s.psend, s.recvc.at[t - ofirst], partner)
     for k, src in enumerate((mp_h, op_h, sp_h)):
@@ -184,7 +184,6 @@
         remote(src, s.ste.at[core, k], s.dsend.at[1], s.drecv.at[1], partner)
 
     x2 = s.x.reshape(SLOTS, 1152, 128)
-    xe2 = s.xE.reshape(SLOTS, 256, 128)
 
     def stage_one(u, x, r1, q, j0, n):
         for d in (1, 3, 2):
@@ -198,12 +197,6 @@
     def keep_one(x, r1, q, j0, n):
         for j in range(j0, j0 + n):
             r1[j, 0] = x[(j,) + cut(q, pos[q])]
-
-    phase("chip_e")
-    got(s.prE.at[pl.ds(0, count)], s.drecv.at[2])
-    for j in range(count):
-        xe2[j] = (eterm(first + j) + s.prE[j].astype(F32)).astype(BF16)
-    stage_one(E, s.xE, s.r1E, *eunit)
 
     for tiles in paired(list(range(first, first + count))):
         phase(f"own_terms{tiles[0] - first}")
@@ -217,9 +210,21 @@
             stage_one(j, s.x, s.r1, *units[j])
 
     phase("keep")
-    keep_one(s.xE, s.r1E, *eunit)
     for unit in units:
         keep_one(s.x, s.r1, *unit)
+
+    phase("embed")
+    ev = s.eb.reshape(TILES + 4, 16, 128)
+    y2e = s.yE.reshape(SLOTS, 64, 128)
+    got(s.eb.at[:, pl.ds(0, 7)], s.drecv.at[2])
+    s.ef[:, 0 : count * 128] = lax.dot_general(
+        jnp.concatenate([ev[TILES], ev[TILES + 1]], axis=1),
+        jnp.concatenate([ev[first + j] for j in range(count)], axis=1),
+        (((0,), (0,)), ((), ())), preferred_element_type=F32,
+    )
+    slab = pl.ds(pl.multiple_of(pos[0] * 64, 64), 64)
+    for j in range(count):
+        y2e[j] = s.ef[slab, j * 128 : j * 128 + 128].astype(BF16)
 
     phase("state")
     loaded(s.st.at[core], 5)
@@ -235,16 +240,16 @@
 
     r1v = s.r1.reshape(SLOTS, 4, 288, 128)
     y2 = s.y.reshape(SLOTS, 288, 128)
-    r1ve = s.r1E.reshape(SLOTS, 4, 64, 128)
-    y2e = s.yE.reshape(SLOTS, 64, 128)
-
-    def stage_two(u, r1, r1v, y, y2, r2, words, q, j0, n):
-        got(r1.at[pl.ds(j0, n), pl.ds(1, 3)], s.recva.at[u])
+
+    def ring_sum(u, q, j0, n):
+        got(s.r1.at[pl.ds(j0, n), pl.ds(1, 3)], s.recva.at[u])
         for j in range(j0, j0 + n):
             total = r1v[j, 0].astype(F32)
             for d in (1, 2, 3):
                 total = total + r1v[j, d].astype(F32)
             y2[j] = total.astype(BF16)
+
+    def stage_two(u, y, r2, words, q, j0, n):
         for a, b in FAR:
             spot = in_plane(q, a, b)
             p1, p2 = plane_of(q, spot)
@@ -257,11 +262,12 @@
         for j in range(j0, j0 + n):
             r2[j, 0, 0:words] = y[j, p1, p2]
 
+    phase("two_e")
+    stage_two(E, s.yE, s.r2E, 2, *eunit)
     for u, unit in enumerate(units):
         phase(f"two{u}")
-        stage_two(u, s.r1, r1v, s.y, y2, s.r2, 9, *unit)
-    phase("two_e")
-    stage_two(E, s.r1E, r1ve, s.yE, y2e, s.r2E, 2, *eunit)
+        ring_sum(u, *unit)
+        stage_two(u, s.y, s.r2, 9, *unit)
 
     r2v = s.r2.reshape(SLOTS, 16, 24, 128)
     r2ve = s.r2E.reshape(SLOTS, 16, 8, 128)
@@ -303,7 +309,6 @@
     sent(s.st.at[core], s.dsend.at[0])
     sent(s.ste.at[core], s.dsend.at[1])
     sent(s.r1.at[pl.ds(0, count), pl.ds(1, 3)], s.senda.at[0])
-    sent(s.r1E.at[pl.ds(0, count), pl.ds(1, 3)], s.senda.at[1])
     sent(s.r2.at[pl.ds(0, count), pl.ds(1, 15), pl.ds(0, 9)], s.sendb.at[0])
     sent(s.r2E.at[pl.ds(0, count), pl.ds(1, 15), pl.ds(0, 2)], s.sendb.at[1])
     phase("norm_b")
@@ -354,21 +359,40 @@
             out[pl.ds(first + j, 9, stride=9), :] = s.dirs[k, j, 9 * core : 9 * core + 9]
             oute[pl.ds(first + j, 2, stride=9), :] = s.dirsE[k, j, 2 * core : 2 * core + 2]
 
-    def ring(u, r2, v, w, words, q, j0, n):
-        got(r2.at[pl.ds(j0, n), pl.ds(1, 15), pl.ds(0, words)], s.recva.at[u])
-        place = w.at[(pl.ds(first + j0, n),) + cut(q, pos[q])]
+    def ring(u, q, j0, n):
+        got(s.r2.at[pl.ds(j0, n), pl.ds(1, 15), pl.ds(0, 9)], s.recva.at[u])
+        place = s.w.at[(pl.ds(first + j0, n),) + cut(q, pos[q])]
         for d in (1, 3, 2):
-            remote(v.at[pl.ds(j0, n)], place, s.sendb.at[int(u == E)], s.recvb.at[u], at(q, d))
-        remote(v.at[pl.ds(j0, n)], place, s.sendc.at[int(u == E)], s.recvc.at[u], partner)
+            remote(s.v.at[pl.ds(j0, n)], place, s.sendb.at[0], s.recvq.at[u, d - 1], at(q, d))
+        remote(s.v.at[pl.ds(j0, n)], place, s.sendc.at[0], s.recvc.at[u], partner)
         for j in range(j0, j0 + n):
-            w[(first + j,) + cut(q, pos[q])] = v[j]
-
-    for u in order:
+            s.w[(first + j,) + cut(q, pos[q])] = s.v[j]
+
+    for u in range(count):
         phase(f"ring{u}")
-        if u == E:
-            ring(E, s.r2E, s.vE, s.wE, 2, *eunit)
-        else:
-            ring(u, s.r2, s.v, s.w, 9, *units[u])
+        ring(u, *units[u])
+
+    phase("ring_e")
+    got(s.r2E.at[pl.ds(0, count), pl.ds(1, 15), pl.ds(0, 2)], s.recva.at[E])
+    v2e = s.vE.reshape(SLOTS, 64, 128)
+    for j in range(count):
+        s.wz[j, slab] = v2e[j]
+    mixed = jnp.dot(
+        jnp.concatenate([ev[TILES + 2], ev[TILES + 3]], axis=1),
+        jnp.concatenate([s.wz[j] for j in range(count)], axis=1),
+        preferred_element_type=F32,
+    )
+    for k in range(8):
+        for j in range(count):
+            s.ep[k, j] = mixed[2 * k : 2 * k + 2, j * 128 : j * 128 + 128]
+    mine = pl.ds(first, count)
+    for spot in beside:
+        remote(
+            s.ep.at[spot[0] * 2 + spot[3], pl.ds(0, count)], s.er.at[pos[0], mine],
+            s.sendc.at[1], s.recvc.at[E], spot,
+        )
+    for j in range(count):
+        s.er[pos[0], first + j] = s.ep[slot, j]
 
     phase("outs2")
     got(s.orr, s.drecv.at[0])
@@ -380,46 +404,56 @@
 
     loaded(s.nxt, 7)
     w2 = s.w.reshape(TILES, 1152, 128)
-    we2 = s.wE.reshape(TILES, 256, 128)
-
-    def own(u, r1, w, q, j0, n):
+
+    def own(u):
         phase(f"own{u}")
-        got(r1.at[pl.ds(j0, n), pl.ds(1, 3)], s.recvb.at[u])
+        q, j0, n = units[u]
         for d in (1, 3, 2):
-            quarter = w.at[(pl.ds(first + j0, n),) + cut(q, at(q, d)[q])]
-            remote(quarter, quarter, s.sendc.at[int(u == E)], s.recvc.at[u], partner)
+            got(s.v.at[pl.ds(j0, n)], s.recvq.at[u, d - 1])
+            quarter = s.w.at[(pl.ds(first + j0, n),) + cut(q, at(q, 4 - d)[q])]
+            remote(quarter, quarter, s.sendc.at[0], s.recvc.at[u], partner)
 
     def theirs(u):
         phase(f"theirs{u}")
         got(s.w.at[ofirst + u], s.recvc.at[u])
 
-    def product(lo, hi):
-        phase(f"product{lo}")
-        whole = jnp.concatenate([w2[t] for t in range(lo, hi)], axis=1)
+    def product(tiles):
+        phase(f"product{tiles[0]}")
+        whole = jnp.concatenate([w2[k] for k in tiles], axis=1)
         for h in range(2):
-            o_np[h * 256 : h * 256 + 256, lo * 128 : hi * 128] = jnp.dot(
-                s.nxt[h * 256 : h * 256 + 256, :], whole, preferred_element_type=F32
-            ).astype(BF16)
-
-    def eproduct(lo, hi):
-        phase(f"eproduct{lo}")
-        whole = jnp.concatenate([we2[t] for t in range(lo, hi)], axis=1)
-        mixed = jnp.dot(waves, whole, preferred_element_type=F32)
-        o_ne[:, lo * 128 : hi * 128] = mixed[2:4].astype(BF16)
-
-    for u in range(count):
-        own(u, s.r1, s.w, *units[u])
-    own(E, s.r1E, s.wE, *eunit)
-    product(first, first + count)
-    eproduct(first, first + count)
-    for u in range(ocount):
-        theirs(u)
-    got(s.wE.at[pl.ds(ofirst, ocount)], s.recvc.at[E])
-    product(ofirst, ofirst + ocount)
-    eproduct(ofirst, ofirst + ocount)
+            some = slice(h * 256, h * 256 + 256)
+            mixed = jnp.dot(s.nxt[some, :], whole, preferred_element_type=F32).astype(BF16)
+            for i, k in enumerate(tiles):
+                o_np[some, k * 128 : k * 128 + 128] = mixed[:, i * 128 : i * 128 + 128]
+
+    own(0)
+    own(1)
+    if core == 1:
+        own(2)
+    product([first, first + 1])
+    for u in range(2 if core == 0 else 3, count):
+        own(u)
+    if core == 0:
+        product([2, 3, 4])
+        for u in range(ocount):
+            theirs(u)
+        product([5, 6, 7, 8])
+    else:
+        theirs(0)
+        theirs(1)
+        product([7, 8, 0, 1])
+    phase("embed_out")
+    got(s.ed.at[pl.ds(0, 3 * count + 4 * ocount)], s.recvc.at[E])
+    for k in range(TILES):
+        total = s.er[0, k] + s.er[1, k] + s.er[2, k] + s.er[3, k]
+        o_ne[:, k * 128 : k * 128 + 128] = total.astype(BF16)
+    if core == 1:
+        for u in (2, 3, 4):
+            theirs(u)
+        product([2, 3, 4])
 
     phase("drain")
-    sent(s.psE.at[pl.ds(0, ocount)], s.dsend.at[2])
+    sent(s.eb.at[:, pl.ds(0, 7)], s.dsend.at[2])
     sent(s.os, s.dsend.at[0])
     sent(s.osE, s.dsend.at[1])
     sent(s.ps.at[pl.ds(0, ocount)], s.psend)
@@ -428,9 +462,8 @@
     sent(s.r2.at[pl.ds(0, count), pl.ds(1, 15), pl.ds(0, 9)], s.senda.at[0])
     sent(s.r2E.at[pl.ds(0, count), pl.ds(1, 15), pl.ds(0, 2)], s.senda.at[1])
     sent(s.r1.at[pl.ds(0, count), pl.ds(1, 3)], s.sendb.at[0])
-    sent(s.r1E.at[pl.ds(0, count), pl.ds(1, 3)], s.sendb.at[1])
     sent(s.w.at[pl.ds(first, count)], s.sendc.at[0])
-    sent(s.wE.at[pl.ds(first, count)], s.sendc.at[1])
+    sent(s.ed.at[pl.ds(0, 7 * count)], s.sendc.at[1])
     phase(None)
 
 
@@ -464,12 +497,8 @@
     ste=pltpu.VMEM((2, 3, 18, 128), F32),
     ps=pltpu.VMEM((SLOTS, 1152, 128), BF16),
     pr=pltpu.VMEM((SLOTS, 1152, 128), BF16),
-    psE=pltpu.VMEM((SLOTS, 256, 128), BF16),
-    prE=pltpu.VMEM((SLOTS, 256, 128), BF16),
     x=pltpu.VMEM((SLOTS, 4, 4, 4, 9, 2, 128), BF16),
-    xE=pltpu.VMEM((SLOTS, 4, 4, 4, 2, 2, 128), BF16),
     r1=pltpu.VMEM((SLOTS, 4, 4, 4, 9, 2, 128), BF16),
-    r1E=pltpu.VMEM((SLOTS, 4, 4, 4, 2, 2, 128), BF16),
     y=pltpu.VMEM((SLOTS, 4, 4, 9, 2, 128), BF16),
     yE=pltpu.VMEM((SLOTS, 4, 4, 2, 2, 128), BF16),
     r2=pltpu.VMEM((SLOTS, 16, 12, 2, 128), BF16),
@@ -485,11 +514,16 @@
     v=pltpu.VMEM((SLOTS, 4, 4, 9, 2, 128), BF16),
     vE=pltpu.VMEM((SLOTS, 4, 4, 2, 2, 128), BF16),
     w=pltpu.VMEM((TILES, 4, 4, 4, 9, 2, 128), BF16),
-    wE=pltpu.VMEM((TILES, 4, 4, 4, 2, 2, 128), BF16),
     os=pltpu.VMEM((2, SLOTS, 16, 128), F32),
     osE=pltpu.VMEM((2, SLOTS, 8, 128), F32),
     orr=pltpu.VMEM((2, SLOTS, 16, 128), F32),
     orrE=pltpu.VMEM((2, SLOTS, 8, 128), F32),
+    eb=pltpu.VMEM((TILES + 4, 8, 2, 128), BF16),
+    ef=pltpu.VMEM((256, 640), F32),
+    wz=pltpu.VMEM((SLOTS, 256, 128), BF16),
+    ep=pltpu.VMEM((8, SLOTS, 2, 128), F32),
+    er=pltpu.VMEM((4, TILES, 2, 128), F32),
+    ed=pltpu.VMEM((36, 2, 128), F32),
     na=pltpu.VMEM((2, 1, 128), F32),
     nb=pltpu.VMEM((4, 4, 4, 1, 128), F32),
     nw=pltpu.VMEM((63, 1, 128), F32),
@@ -500,6 +534,7 @@
     senda=DMA((2,)),
     sendb=DMA((2,)),
     sendc=DMA((2,)),
+    recvq=DMA((5, 3)),
     recva=DMA((6,)),
     recvb=DMA((6,)),
     recvc=DMA((6,)),

time: 51.4 us -> 49.4 us (0.961)
  Pallas kernels: 50.5 us -> 48.5 us
    pallas_call x1, Pallas kernels: 49.4 us -> 47.4 us  [shards(): pl.pallas_call(kernel, out_shape=[pltpu.VMEM(r.shape, r.dtype) for r in r...]
where the time goes in v5:
time: 49.4 us; the launch traced here: 49.3 us
  Pallas kernels  48.5 us (98%)
  between operations  0.81 us (2%)
    pallas_call x1, Pallas kernels, shards(): pl.pallas_call(kernel, out_shape=[pltpu.VMEM(r.shape, r.dtype) for r in r...  47.4 us
    pallas_call x1, Pallas kernels, shards(): pl.pallas_call(write_out, out_shape=results, in_specs=[vmem] * 7, out_spe...  1.1 us

profile of v5, /device:TPU:1, one launch (start us, length us, event | category | flops | bytes accessed | tf_op | source)
XLA Modules:
  0.0 49.3 jit_solution(11341009623053009493)
XLA Ops:
  0.6 47.4 %step.1 = (bf16[512,1152]{1,0:T(8,128)(2,1)S(1)}, bf16[2,1152]{1,0:T(2,128)(2,1)S(1)}, f32[81,128]{1,0:T(8,128)S(1)}, f32[18,128]{1,0:T(8,128)S(1)}, f32[81,128]...) custom-call(bf16[512,1152]{1,0:T(8,128)(2,1)} %refs_0_.1, bf16[512,1152]{1,0:T(8,128)(2,1)} %refs_1_.1, ...), custom_call_target="tpu_custom_call" | custom-call | tf_op jit(solution)/shard_map/step/pallas_call | solution.py:582
  48.0 1.1 %write_out.1 = (bf16[512,1152]{1,0:T(8,128)(2,1)}, bf16[2,1152]{1,0:T(2,128)(2,1)}, f32[81,128]{1,0:T(8,128)}, f32[18,128]{1,0:T(8,128)}, f32[81,128]{1,0:T(8,12...) custom-call(bf16[512,1152]{1,0:T(8,128)(2,1)S(1)} %get-tuple-element.21.refs_0_, bf16[2,1152]{1,0:T(2,128)(2,1)S(1)} %get-tuple-element.22.refs_1_, ...), custom_call_target="tpu_custom_call" | custom-call | tf_op jit(solution)/shard_map/write_out/pallas_call | solution.py:593

commit v6 on v5

--- a/solution.py
+++ b/solution.py
@@ -198,14 +198,17 @@
         for j in range(j0, j0 + n):
             r1[j, 0] = x[(j,) + cut(q, pos[q])]
 
-    for tiles in paired(list(range(first, first + count))):
-        phase(f"own_terms{tiles[0] - first}")
-        parts = terms(tiles)
+    groups = paired(list(range(first, first + count)))
+    parts = {0: terms(groups[0])}
+    for g, tiles in enumerate(groups):
+        phase(f"own_terms{g}")
+        if g + 1 < len(groups):
+            parts[g + 1] = terms(groups[g + 1])
         for i, t in enumerate(tiles):
             j = t - first
             got(s.pr.at[j], s.recvc.at[j])
             for h in range(2):
-                part = parts[h][:, i * 128 : i * 128 + 128]
+                part = parts[g][h][:, i * 128 : i * 128 + 128]
                 x2[j, h * 576 : h * 576 + 576] = (part + s.pr[j, h * 576 : h * 576 + 576].astype(F32)).astype(BF16)
             stage_one(j, s.x, s.r1, *units[j])
 
@@ -426,31 +429,38 @@
             for i, k in enumerate(tiles):
                 o_np[some, k * 128 : k * 128 + 128] = mixed[:, i * 128 : i * 128 + 128]
 
+    def embed_out():
+        phase("embed_out")
+        got(s.ed.at[pl.ds(0, 3 * count + 4 * ocount)], s.recvc.at[E])
+        for k in range(TILES):
+            total = s.er[0, k] + s.er[1, k] + s.er[2, k] + s.er[3, k]
+            o_ne[:, k * 128 : k * 128 + 128] = total.astype(BF16)
+
     own(0)
     own(1)
-    if core == 1:
+    if core == 0:
+        product([0, 1])
+        own(3)
+        own(4)
         own(2)
-    product([first, first + 1])
-    for u in range(2 if core == 0 else 3, count):
-        own(u)
-    if core == 0:
         product([2, 3, 4])
+        embed_out()
         for u in range(ocount):
             theirs(u)
         product([5, 6, 7, 8])
     else:
+        own(2)
+        product([5, 6])
+        own(3)
         theirs(0)
         theirs(1)
         product([7, 8, 0, 1])
-    phase("embed_out")
-    got(s.ed.at[pl.ds(0, 3 * count + 4 * ocount)], s.recvc.at[E])
-    for k in range(TILES):
-        total = s.er[0, k] + s.er[1, k] + s.er[2, k] + s.er[3, k]
-        o_ne[:, k * 128 : k * 128 + 128] = total.astype(BF16)
-    if core == 1:
-        for u in (2, 3, 4):
-            theirs(u)
-        product([2, 3, 4])
+        embed_out()
+        theirs(3)
+        theirs(4)
+        product([3, 4])
+        theirs(2)
+        product([2])
 
     phase("drain")
     sent(s.eb.at[:, pl.ds(0, 7)], s.dsend.at[2])

time: 49.4 us -> 48.3 us (0.978)
  Pallas kernels: 48.5 us -> 47.3 us
    pallas_call x1, Pallas kernels: 47.4 us -> 46.2 us  [shards(): pl.pallas_call(kernel, out_shape=[pltpu.VMEM(r.shape, r.dtype) for r in r...]
where the time goes in v6:
time: 48.3 us; the launch traced here: 48.1 us
  Pallas kernels  47.3 us (98%)
  between operations  0.81 us (2%)
    pallas_call x1, Pallas kernels, shards(): pl.pallas_call(kernel, out_shape=[pltpu.VMEM(r.shape, r.dtype) for r in r...  46.2 us
    pallas_call x1, Pallas kernels, shards(): pl.pallas_call(write_out, out_shape=results, in_specs=[vmem] * 7, out_spe...  1.1 us

profile of v6, /device:TPU:1, one launch (start us, length us, event | category | flops | bytes accessed | tf_op | source)
XLA Modules:
  0.0 48.1 jit_solution(2912876879683276079)
XLA Ops:
  0.6 46.2 %step.1 = (bf16[512,1152]{1,0:T(8,128)(2,1)S(1)}, bf16[2,1152]{1,0:T(2,128)(2,1)S(1)}, f32[81,128]{1,0:T(8,128)S(1)}, f32[18,128]{1,0:T(8,128)S(1)}, f32[81,128]...) custom-call(bf16[512,1152]{1,0:T(8,128)(2,1)} %refs_0_.1, bf16[512,1152]{1,0:T(8,128)(2,1)} %refs_1_.1, ...), custom_call_target="tpu_custom_call" | custom-call | tf_op jit(solution)/shard_map/step/pallas_call | solution.py:592
  46.9 1.1 %write_out.1 = (bf16[512,1152]{1,0:T(8,128)(2,1)}, bf16[2,1152]{1,0:T(2,128)(2,1)}, f32[81,128]{1,0:T(8,128)}, f32[18,128]{1,0:T(8,128)}, f32[81,128]{1,0:T(8,12...) custom-call(bf16[512,1152]{1,0:T(8,128)(2,1)S(1)} %get-tuple-element.21.refs_0_, bf16[2,1152]{1,0:T(2,128)(2,1)S(1)} %get-tuple-element.22.refs_1_, ...), custom_call_target="tpu_custom_call" | custom-call | tf_op jit(solution)/shard_map/write_out/pallas_call | solution.py:603

commit v7 on v6

--- a/solution.py
+++ b/solution.py
@@ -202,15 +202,17 @@
     parts = {0: terms(groups[0])}
     for g, tiles in enumerate(groups):
         phase(f"own_terms{g}")
+        for t in tiles:
+            got(s.pr.at[t - first], s.recvc.at[t - first])
         if g + 1 < len(groups):
             parts[g + 1] = terms(groups[g + 1])
         for i, t in enumerate(tiles):
             j = t - first
-            got(s.pr.at[j], s.recvc.at[j])
             for h in range(2):
                 part = parts[g][h][:, i * 128 : i * 128 + 128]
                 x2[j, h * 576 : h * 576 + 576] = (part + s.pr[j, h * 576 : h * 576 + 576].astype(F32)).astype(BF16)
-            stage_one(j, s.x, s.r1, *units[j])
+        for t in tiles:
+            stage_one(t - first, s.x, s.r1, *units[t - first])
 
     phase("keep")
     for unit in units:
@@ -276,6 +278,16 @@
     r2ve = s.r2E.reshape(SLOTS, 16, 8, 128)
     squares = jnp.zeros((24, 128), F32)
     squares_e = jnp.zeros((8, 128), F32)
+    phase("sum_e")
+    q, j0, n = eunit
+    got(s.r2E.at[pl.ds(j0, n), pl.ds(1, 15), pl.ds(0, 2)], s.recvb.at[E])
+    for j in range(j0, j0 + n):
+        total = r2ve[j, 0].astype(F32)
+        for k in range(1, 16):
+            total = total + r2ve[j, k].astype(F32)
+        s.gE[j] = total
+        squares_e = squares_e + total * total
+
     for u, (q, j0, n) in enumerate(units):
         phase(f"sum{u}")
         got(s.r2.at[pl.ds(j0, n), pl.ds(1, 15), pl.ds(0, 9)], s.recvb.at[u])
@@ -285,16 +297,6 @@
                 total = total + r2v[j, k].astype(F32)
             s.g[j] = total
             squares = squares + total * total
-    phase("sum_e")
-    q, j0, n = eunit
-    got(s.r2E.at[pl.ds(j0, n), pl.ds(1, 15), pl.ds(0, 2)], s.recvb.at[E])
-    for j in range(j0, j0 + n):
-        total = r2ve[j, 0].astype(F32)
-        for k in range(1, 16):
-            total = total + r2ve[j, k].astype(F32)
-        s.gE[j] = total
-        squares_e = squares_e + total * total
-
     phase("squares")
     rows = lax.broadcasted_iota(jnp.int32, (24, 128), 0)
     rows_e = lax.broadcasted_iota(jnp.int32, (8, 128), 0)
@@ -316,9 +318,10 @@
     sent(s.r2E.at[pl.ds(0, count), pl.ds(1, 15), pl.ds(0, 2)], s.sendb.at[1])
     phase("norm_b")
     got(s.nw, s.nrecv.at[1])
-    total = s.nb[0, 0, 0]
-    for k in range(1, 64):
-        total = total + s.nb[k // 16, k // 4 % 4, k % 4]
+    level = [s.nb[k // 16, k // 4 % 4, k % 4] for k in range(64)]
+    while len(level) > 1:
+        level = [a + b for a, b in zip(level[::2], level[1::2])]
+    total = level[0]
     grad_norm = jnp.sqrt(jnp.sum(total, axis=1, keepdims=True))
     clip = jnp.minimum(jnp.float32(1.0), max_norm / (grad_norm + 1e-06))
     o_norm[...] = jnp.broadcast_to(grad_norm, (1, 128))
@@ -423,8 +426,9 @@
     def product(tiles):
         phase(f"product{tiles[0]}")
         whole = jnp.concatenate([w2[k] for k in tiles], axis=1)
-        for h in range(2):
-            some = slice(h * 256, h * 256 + 256)
+        halves = 2 if len(tiles) < 3 else 1
+        for h in range(halves):
+            some = slice(h * 256, h * 256 + 512 // halves)
             mixed = jnp.dot(s.nxt[some, :], whole, preferred_element_type=F32).astype(BF16)
             for i, k in enumerate(tiles):
                 o_np[some, k * 128 : k * 128 + 128] = mixed[:, i * 128 : i * 128 + 128]
@@ -436,31 +440,38 @@
             total = s.er[0, k] + s.er[1, k] + s.er[2, k] + s.er[3, k]
             o_ne[:, k * 128 : k * 128 + 128] = total.astype(BF16)
 
+    def many(base, *tiles):
+        product([base + k for k in tiles])
+
     own(0)
     own(1)
-    if core == 0:
-        product([0, 1])
+    if count == 5:
+        many(first, 0, 1)
+        theirs(0)
+        theirs(1)
+        many(ofirst, 0, 1)
         own(3)
         own(4)
         own(2)
-        product([2, 3, 4])
+        many(first, 2, 3, 4)
         embed_out()
-        for u in range(ocount):
-            theirs(u)
-        product([5, 6, 7, 8])
+        theirs(2)
+        theirs(3)
+        many(ofirst, 2, 3)
     else:
         own(2)
-        product([5, 6])
-        own(3)
+        many(first, 0, 1, 2)
         theirs(0)
         theirs(1)
-        product([7, 8, 0, 1])
+        many(ofirst, 0, 1)
+        own(3)
+        many(first, 3)
         embed_out()
         theirs(3)
         theirs(4)
-        product([3, 4])
+        many(ofirst, 3, 4)
         theirs(2)
-        product([2])
+        many(ofirst, 2)
 
     phase("drain")
     sent(s.eb.at[:, pl.ds(0, 7)], s.dsend.at[2])

time: 48.3 us -> 48.2 us (level)
  no operation moved by 1% of the time
where the time goes in v7:
time: 48.2 us; the launch traced here: 48 us
  Pallas kernels  47.2 us (98%)
  between operations  0.81 us (2%)
    pallas_call x1, Pallas kernels, shards(): pl.pallas_call(kernel, out_shape=[pltpu.VMEM(r.shape, r.dtype) for r in r...  46.1 us
    pallas_call x1, Pallas kernels, shards(): pl.pallas_call(write_out, out_shape=results, in_specs=[vmem] * 7, out_spe...  1.1 us

profile of v7, /device:TPU:1, one launch (start us, length us, event | category | flops | bytes accessed | tf_op | source)
XLA Modules:
  0.0 48.0 jit_solution(1926662224287817466)
XLA Ops:
  0.6 46.1 %step.1 = (bf16[512,1152]{1,0:T(8,128)(2,1)S(1)}, bf16[2,1152]{1,0:T(2,128)(2,1)S(1)}, f32[81,128]{1,0:T(8,128)S(1)}, f32[18,128]{1,0:T(8,128)S(1)}, f32[81,128]...) custom-call(bf16[512,1152]{1,0:T(8,128)(2,1)} %refs_0_.1, bf16[512,1152]{1,0:T(8,128)(2,1)} %refs_1_.1, ...), custom_call_target="tpu_custom_call" | custom-call | tf_op jit(solution)/shard_map/step/pallas_call | solution.py:603
  46.8 1.1 %write_out.1 = (bf16[512,1152]{1,0:T(8,128)(2,1)}, bf16[2,1152]{1,0:T(2,128)(2,1)}, f32[81,128]{1,0:T(8,128)}, f32[18,128]{1,0:T(8,128)}, f32[81,128]{1,0:T(8,12...) custom-call(bf16[512,1152]{1,0:T(8,128)(2,1)S(1)} %get-tuple-element.21.refs_0_, bf16[2,1152]{1,0:T(2,128)(2,1)S(1)} %get-tuple-element.22.refs_1_, ...), custom_call_target="tpu_custom_call" | custom-call | tf_op jit(solution)/shard_map/write_out/pallas_call | solution.py:614

commit v8 on v7

--- a/solution.py
+++ b/solution.py
@@ -121,7 +121,8 @@
         tuple(lax.rem(pos[k] + d[k], 4) for k in range(3)) + (pos[3],) for d in AROUND
     ]
     beside = [tuple(at(0, d)[:3]) + (c,) for d in range(4) for c in (core, other)][1:]
-    everyone = around + [spot for spot in beside if spot[3] == other]
+    rings = [tuple(at(q, d)) for q in range(3) for d in (2, 1, 3)]
+    everyone = rings + [spot for spot in beside if spot[3] == other]
     for spot in everyone:
         pl.semaphore_signal(barrier, inc=1, device_id=spot, device_id_type=MESH)
 
@@ -267,12 +268,15 @@
         for j in range(j0, j0 + n):
             r2[j, 0, 0:words] = y[j, p1, p2]
 
-    phase("two_e")
-    stage_two(E, s.yE, s.r2E, 2, *eunit)
     for u, unit in enumerate(units):
         phase(f"two{u}")
         ring_sum(u, *unit)
-        stage_two(u, s.y, s.r2, 9, *unit)
+        if u == 1:
+            stage_two(0, s.y, s.r2, 9, *units[0])
+        if u > 0:
+            stage_two(u, s.y, s.r2, 9, *unit)
+        if u == 1:
+            stage_two(E, s.yE, s.r2E, 2, *eunit)
 
     r2v = s.r2.reshape(SLOTS, 16, 24, 128)
     r2ve = s.r2E.reshape(SLOTS, 16, 8, 128)

time: 48.2 us -> 46.8 us (0.971)
  Pallas kernels: 47.2 us -> 45.9 us
    pallas_call x1, Pallas kernels: 46.1 us -> 44.8 us  [shards(): pl.pallas_call(kernel, out_shape=[pltpu.VMEM(r.shape, r.dtype) for r in r...]
where the time goes in v8:
time: 46.8 us; the launch traced here: 46.7 us
  Pallas kernels  45.9 us (98%)
  between operations  0.81 us (2%)
    pallas_call x1, Pallas kernels, shards(): pl.pallas_call(kernel, out_shape=[pltpu.VMEM(r.shape, r.dtype) for r in r...  44.8 us
    pallas_call x1, Pallas kernels, shards(): pl.pallas_call(write_out, out_shape=results, in_specs=[vmem] * 7, out_spe...  1.1 us

profile of v8, /device:TPU:1, one launch (start us, length us, event | category | flops | bytes accessed | tf_op | source)
XLA Modules:
  0.0 46.7 jit_solution(10955162753926268568)
XLA Ops:
  0.6 44.8 %step.1 = (bf16[512,1152]{1,0:T(8,128)(2,1)S(1)}, bf16[2,1152]{1,0:T(2,128)(2,1)S(1)}, f32[81,128]{1,0:T(8,128)S(1)}, f32[18,128]{1,0:T(8,128)S(1)}, f32[81,128]...) custom-call(bf16[512,1152]{1,0:T(8,128)(2,1)} %refs_0_.1, bf16[512,1152]{1,0:T(8,128)(2,1)} %refs_1_.1, ...), custom_call_target="tpu_custom_call" | custom-call | tf_op jit(solution)/shard_map/step/pallas_call | solution.py:607
  45.4 1.1 %write_out.1 = (bf16[512,1152]{1,0:T(8,128)(2,1)}, bf16[2,1152]{1,0:T(2,128)(2,1)}, f32[81,128]{1,0:T(8,128)}, f32[18,128]{1,0:T(8,128)}, f32[81,128]{1,0:T(8,12...) custom-call(bf16[512,1152]{1,0:T(8,128)(2,1)S(1)} %get-tuple-element.21.refs_0_, bf16[2,1152]{1,0:T(2,128)(2,1)S(1)} %get-tuple-element.22.refs_1_, ...), custom_call_target="tpu_custom_call" | custom-call | tf_op jit(solution)/shard_map/write_out/pallas_call | solution.py:618

commit v9 on v8

--- a/solution.py
+++ b/solution.py
@@ -35,6 +35,7 @@
 FAR = [(a, b) for a in (2, 1, 3, 0) for b in (2, 1, 3, 0) if (a, b) != (0, 0)]
 EUNIT = {0: (0, 0, 5), 1: (0, 0, 4)}
 SLOTS = 5
+LATE = {0: (7, 8), 1: (2,)}
 PHASES = False
 
 
@@ -51,7 +52,7 @@
 
 def body(core, hbm, outs, sc):
     (att_h, cot_h, nxt_h, mp_h, op_h, sp_h, me_h, oe_h, se_h, tn_h, tx_h, ec_h) = hbm
-    (o_np, o_ne, o_dir, o_dire, o_mst, o_mste, o_norm) = outs
+    (o_np, o_ne, o_dir, o_dire, o_mst, o_mste, o_norm) = outs[:7]
     s = sc
     pos = [lax.axis_index(a) for a in AXES]
     other = 1 - core
@@ -461,7 +462,6 @@
         embed_out()
         theirs(2)
         theirs(3)
-        many(ofirst, 2, 3)
     else:
         own(2)
         many(first, 0, 1, 2)
@@ -475,7 +475,6 @@
         theirs(4)
         many(ofirst, 3, 4)
         theirs(2)
-        many(ofirst, 2)
 
     phase("drain")
     sent(s.eb.at[:, pl.ds(0, 7)], s.dsend.at[2])
@@ -514,7 +513,6 @@
     att=pltpu.VMEM((512, 1152), BF16),
     attT=pltpu.VMEM((1152, 512), BF16),
     cot=pltpu.VMEM((512, 1152), BF16),
-    nxt=pltpu.VMEM((512, 1152), BF16),
     ecot=pltpu.VMEM((2, 1152), BF16),
     now=pltpu.SMEM((2,), F32),
     later=pltpu.SMEM((2,), F32),
@@ -538,7 +536,6 @@
     zE=pltpu.VMEM((SLOTS, 4, 2, 128), BF16),
     v=pltpu.VMEM((SLOTS, 4, 4, 9, 2, 128), BF16),
     vE=pltpu.VMEM((SLOTS, 4, 4, 2, 2, 128), BF16),
-    w=pltpu.VMEM((TILES, 4, 4, 4, 9, 2, 128), BF16),
     os=pltpu.VMEM((2, SLOTS, 16, 128), F32),
     osE=pltpu.VMEM((2, SLOTS, 8, 128), F32),
     orr=pltpu.VMEM((2, SLOTS, 16, 128), F32),
@@ -569,10 +566,11 @@
 
 
 def kernel(*refs):
-    hbm, outs, scratch = refs[:12], refs[12:19], refs[19:]
+    hbm, outs, scratch = refs[:12], refs[12:21], refs[21:]
     s = Names()
     for name, ref in zip(SCRATCH, scratch, strict=True):
         setattr(s, name, ref)
+    s.w, s.nxt = outs[7:]
     core = lax.axis_index("c")
     for k in (0, 1):
 
@@ -582,12 +580,34 @@
 
 
 def write_out(*refs):
-    sems = refs[14]
-    copies = [pltpu.make_async_copy(refs[k], refs[7 + k], sems.at[k]) for k in range(7)]
-    for copy in copies:
-        copy.start()
-    for copy in copies:
-        copy.wait()
+    ins, outs, (sems, late_sem, buffer) = refs[:9], refs[9:16], refs[16:]
+    proj, w, nxt = ins[0], ins[7].reshape(TILES, 1152, 128), ins[8]
+    small = [pltpu.make_async_copy(ins[k], outs[k], sems.at[k]) for k in range(1, 7)]
+    core = lax.axis_index("c")
+    for k in (0, 1):
+
+        @pl.when(core == k)
+        def _():
+            low, high = LATE[k][0] * 128, (LATE[k][-1] + 1) * 128
+            done = [cols for cols in (slice(0, low), slice(high, 1152)) if cols.start < cols.stop]
+            copies = [
+                pltpu.make_async_copy(proj.at[:, cols], outs[0].at[:, cols], sems.at[7 * i])
+                for i, cols in enumerate(done)
+            ] + small
+            for copy in copies:
+                copy.start()
+            whole = jnp.concatenate([w[tile] for tile in LATE[k]], axis=1)
+            for h in range(2):
+                some = slice(h * 256, h * 256 + 256)
+                buffer[some, 0 : high - low] = jnp.dot(
+                    nxt[some, :], whole, preferred_element_type=F32
+                ).astype(BF16)
+            last = pltpu.make_async_copy(
+                buffer.at[:, 0 : high - low], outs[0].at[:, low:high], late_sem
+            )
+            last.start()
+            for copy in copies + [last]:
+                copy.wait()
 
 
 def shards(
@@ -604,23 +624,24 @@
         shape((512, 1152), BF16), shape((2, 1152), BF16), shape((81, 128), F32),
         shape((18, 128), F32), shape((81, 128), F32), shape((18, 128), F32), shape((1, 128), F32),
     )
+    passed = (shape((TILES, 4, 4, 4, 9, 2, 128), BF16), shape((512, 1152), BF16))
     inside = pl.pallas_call(
         kernel,
-        out_shape=[pltpu.VMEM(r.shape, r.dtype) for r in results],
+        out_shape=[pltpu.VMEM(r.shape, r.dtype) for r in results + passed],
         in_specs=[large] * 12,
-        out_specs=[vmem] * 7,
+        out_specs=[vmem] * 9,
         scratch_shapes=list(SCRATCH.values()),
         compiler_params=pltpu.CompilerParams(
-            collective_id=0, has_side_effects=True, vmem_limit_bytes=60 * 2**20
+            collective_id=0, has_side_effects=True, vmem_limit_bytes=58 * 2**20
         ),
         name="step",
     )(attended, proj_cot, attended_next, *flat, *flat_e, timesteps, timesteps_next, embed_cot)
     nproj, nembed, d, de, m, mste, norm = pl.pallas_call(
         write_out,
         out_shape=results,
-        in_specs=[vmem] * 7,
+        in_specs=[vmem] * 9,
         out_specs=[large] * 7,
-        scratch_shapes=[DMA((7,))],
+        scratch_shapes=[DMA((8,)), DMA(()), pltpu.VMEM((512, 256), BF16)],
         compiler_params=pltpu.CompilerParams(vmem_limit_bytes=8 * 2**20),
         name="write_out",
     )(*inside)

time: 46.8 us -> 46.6 us (level)
    pallas_call x1, Pallas kernels: 44.8 us -> 44.3 us  [shards(): pl.pallas_call(kernel, out_shape=[pltpu.VMEM(r.shape, r.dtype) for r in r...]
where the time goes in v9:
time: 46.6 us; the launch traced here: 46.4 us
  Pallas kernels  45.6 us (98%)
  between operations  0.81 us (2%)
    pallas_call x1, Pallas kernels, shards(): pl.pallas_call(kernel, out_shape=[pltpu.VMEM(r.shape, r.dtype) for r in r...  44.3 us
    pallas_call x1, Pallas kernels, shards(): pl.pallas_call(write_out, out_shape=results, in_specs=[vmem] * 9, out_spe...  1.32 us

profile of v9, /device:TPU:1, one launch (start us, length us, event | category | flops | bytes accessed | tf_op | source)
XLA Modules:
  0.0 46.4 jit_solution(1400090584186186451)
XLA Ops:
  0.6 44.3 %step.1 = (bf16[512,1152]{1,0:T(8,128)(2,1)S(1)}, bf16[2,1152]{1,0:T(2,128)(2,1)S(1)}, f32[81,128]{1,0:T(8,128)S(1)}, f32[18,128]{1,0:T(8,128)S(1)}, f32[81,128]...) custom-call(bf16[512,1152]{1,0:T(8,128)(2,1)} %refs_0_.1, ...), custom_call_target="tpu_custom_call" | custom-call | tf_op jit(solution)/shard_map/step/pallas_call | solution.py:628
  44.9 1.3 %write_out.1 = (bf16[512,1152]{1,0:T(8,128)(2,1)}, bf16[2,1152]{1,0:T(2,128)(2,1)}, f32[81,128]{1,0:T(8,128)}, f32[18,128]{1,0:T(8,128)}, f32[81,128]{1,0:T(8,12...) custom-call(bf16[512,1152]{1,0:T(8,128)(2,1)S(1)} %get-tuple-element.23.refs_0_, bf16[2,1152]{1,0:T(2,128)(2,1)S(1)} %get-tuple-element.24.refs_1_, ...), custom_call_target="tpu_custom_call" | custom-call | tf_op jit(solution)/shard_map/write_out/pallas_call | solution.py:639

commit v10 on v9

--- a/solution.py
+++ b/solution.py
@@ -35,7 +35,7 @@
 FAR = [(a, b) for a in (2, 1, 3, 0) for b in (2, 1, 3, 0) if (a, b) != (0, 0)]
 EUNIT = {0: (0, 0, 5), 1: (0, 0, 4)}
 SLOTS = 5
-LATE = {0: (7, 8), 1: (2,)}
+LATE = {0: (7, 8), 1: (2, 4)}
 PHASES = False
 
 
@@ -193,7 +193,7 @@
             remote(
                 x.at[(pl.ds(j0, n),) + cut(q, spot[q])],
                 r1.at[pl.ds(j0, n), d],
-                s.senda.at[int(u == E)], s.recva.at[u], spot,
+                s.senda, s.recva.at[u], spot,
             )
 
     def keep_one(x, r1, q, j0, n):
@@ -263,7 +263,7 @@
             remote(
                 y.at[pl.ds(j0, n), p1, p2],
                 r2.at[pl.ds(j0, n), a * 4 + b, pl.ds(0, words)],
-                s.sendb.at[int(u == E)], s.recvb.at[u], spot,
+                s.sende if u == E else s.sendb, s.recva.at[E] if u == E else s.recvb.at[u], spot,
             )
         p1, p2 = plane_of(q, pos)
         for j in range(j0, j0 + n):
@@ -285,7 +285,7 @@
     squares_e = jnp.zeros((8, 128), F32)
     phase("sum_e")
     q, j0, n = eunit
-    got(s.r2E.at[pl.ds(j0, n), pl.ds(1, 15), pl.ds(0, 2)], s.recvb.at[E])
+    got(s.r2E.at[pl.ds(j0, n), pl.ds(1, 15), pl.ds(0, 2)], s.recva.at[E])
     for j in range(j0, j0 + n):
         total = r2ve[j, 0].astype(F32)
         for k in range(1, 16):
@@ -318,9 +318,10 @@
         remote(mine, mine, s.nsend.at[1], s.nrecv.at[1], spot)
     sent(s.st.at[core], s.dsend.at[0])
     sent(s.ste.at[core], s.dsend.at[1])
-    sent(s.r1.at[pl.ds(0, count), pl.ds(1, 3)], s.senda.at[0])
-    sent(s.r2.at[pl.ds(0, count), pl.ds(1, 15), pl.ds(0, 9)], s.sendb.at[0])
-    sent(s.r2E.at[pl.ds(0, count), pl.ds(1, 15), pl.ds(0, 2)], s.sendb.at[1])
+    sent(s.r1.at[pl.ds(0, count), pl.ds(1, 3)], s.senda)
+    sent(s.r2.at[pl.ds(0, count), pl.ds(1, 15), pl.ds(0, 9)], s.sendb)
+    sent(s.r2E.at[pl.ds(0, count), pl.ds(1, 15), pl.ds(0, 2)], s.sende)
+    sent(s.eb.at[:, pl.ds(0, 7)], s.dsend.at[2])
     phase("norm_b")
     got(s.nw, s.nrecv.at[1])
     level = [s.nb[k // 16, k // 4 % 4, k % 4] for k in range(64)]
@@ -345,7 +346,7 @@
             remote(
                 zz.at[pl.ds(j0, n), pl.ds(0, words)],
                 v.at[pl.ds(j0, n), p1, p2],
-                s.senda.at[int(u == E)], s.recva.at[u], in_plane(q, a, b),
+                s.sende if u == E else s.senda, s.recva.at[u], in_plane(q, a, b),
             )
         for j in range(j0, j0 + n):
             v[j, p1, p2] = zz[j, 0:words]
@@ -374,8 +375,8 @@
         got(s.r2.at[pl.ds(j0, n), pl.ds(1, 15), pl.ds(0, 9)], s.recva.at[u])
         place = s.w.at[(pl.ds(first + j0, n),) + cut(q, pos[q])]
         for d in (1, 3, 2):
-            remote(s.v.at[pl.ds(j0, n)], place, s.sendb.at[0], s.recvq.at[u, d - 1], at(q, d))
-        remote(s.v.at[pl.ds(j0, n)], place, s.sendc.at[0], s.recvc.at[u], partner)
+            remote(s.v.at[pl.ds(j0, n)], place, s.sendb, s.recvq.at[u, int(d == 2)], at(q, d))
+        remote(s.v.at[pl.ds(j0, n)], place, s.sendc, s.recvc.at[u], partner)
         for j in range(j0, j0 + n):
             s.w[(first + j,) + cut(q, pos[q])] = s.v[j]
 
@@ -400,7 +401,7 @@
     for spot in beside:
         remote(
             s.ep.at[spot[0] * 2 + spot[3], pl.ds(0, count)], s.er.at[pos[0], mine],
-            s.sendc.at[1], s.recvc.at[E], spot,
+            s.dsend.at[2], s.drecv.at[2], spot,
         )
     for j in range(count):
         s.er[pos[0], first + j] = s.ep[slot, j]
@@ -419,10 +420,11 @@
     def own(u):
         phase(f"own{u}")
         q, j0, n = units[u]
-        for d in (1, 3, 2):
-            got(s.v.at[pl.ds(j0, n)], s.recvq.at[u, d - 1])
-            quarter = s.w.at[(pl.ds(first + j0, n),) + cut(q, at(q, 4 - d)[q])]
-            remote(quarter, quarter, s.sendc.at[0], s.recvc.at[u], partner)
+        for k, ds in enumerate(((1, 3), (2,))):
+            got(s.r1.at[pl.ds(j0, n), pl.ds(1, len(ds))], s.recvq.at[u, k])
+            for d in ds:
+                quarter = s.w.at[(pl.ds(first + j0, n),) + cut(q, at(q, 4 - d)[q])]
+                remote(quarter, quarter, s.sendc, s.recvc.at[u], partner)
 
     def theirs(u):
         phase(f"theirs{u}")
@@ -440,7 +442,7 @@
 
     def embed_out():
         phase("embed_out")
-        got(s.ed.at[pl.ds(0, 3 * count + 4 * ocount)], s.recvc.at[E])
+        got(s.ed.at[pl.ds(0, 3 * count + 4 * ocount)], s.drecv.at[2])
         for k in range(TILES):
             total = s.er[0, k] + s.er[1, k] + s.er[2, k] + s.er[3, k]
             o_ne[:, k * 128 : k * 128 + 128] = total.astype(BF16)
@@ -472,22 +474,21 @@
         many(first, 3)
         embed_out()
         theirs(3)
+        many(ofirst, 3)
         theirs(4)
-        many(ofirst, 3, 4)
         theirs(2)
 
     phase("drain")
-    sent(s.eb.at[:, pl.ds(0, 7)], s.dsend.at[2])
     sent(s.os, s.dsend.at[0])
     sent(s.osE, s.dsend.at[1])
     sent(s.ps.at[pl.ds(0, ocount)], s.psend)
     sent(s.na.at[core], s.nsend.at[0])
     sent(s.nw, s.nsend.at[1])
-    sent(s.r2.at[pl.ds(0, count), pl.ds(1, 15), pl.ds(0, 9)], s.senda.at[0])
-    sent(s.r2E.at[pl.ds(0, count), pl.ds(1, 15), pl.ds(0, 2)], s.senda.at[1])
-    sent(s.r1.at[pl.ds(0, count), pl.ds(1, 3)], s.sendb.at[0])
-    sent(s.w.at[pl.ds(first, count)], s.sendc.at[0])
-    sent(s.ed.at[pl.ds(0, 7 * count)], s.sendc.at[1])
+    sent(s.r2.at[pl.ds(0, count), pl.ds(1, 15), pl.ds(0, 9)], s.senda)
+    sent(s.r2E.at[pl.ds(0, count), pl.ds(1, 15), pl.ds(0, 2)], s.sende)
+    sent(s.r1.at[pl.ds(0, count), pl.ds(1, 3)], s.sendb)
+    sent(s.w.at[pl.ds(first, count)], s.sendc)
+    sent(s.ed.at[pl.ds(0, 7 * count)], s.dsend.at[2])
     phase(None)
 
 
@@ -553,13 +554,14 @@
     dsend=DMA((3,)),
     drecv=DMA((3,)),
     psend=DMA(()),
-    senda=DMA((2,)),
-    sendb=DMA((2,)),
-    sendc=DMA((2,)),
-    recvq=DMA((5, 3)),
+    senda=DMA(()),
+    sendb=DMA(()),
+    sendc=DMA(()),
+    sende=DMA(()),
+    recvq=DMA((5, 2)),
     recva=DMA((6,)),
-    recvb=DMA((6,)),
-    recvc=DMA((6,)),
+    recvb=DMA((5,)),
+    recvc=DMA((5,)),
     nsend=DMA((2,)),
     nrecv=DMA((2,)),
 )
@@ -580,33 +582,37 @@
 
 
 def write_out(*refs):
-    ins, outs, (sems, late_sem, buffer) = refs[:9], refs[9:16], refs[16:]
+    ins, outs, (sems, buffer) = refs[:9], refs[9:16], refs[16:]
     proj, w, nxt = ins[0], ins[7].reshape(TILES, 1152, 128), ins[8]
-    small = [pltpu.make_async_copy(ins[k], outs[k], sems.at[k]) for k in range(1, 7)]
+    small = [pltpu.make_async_copy(ins[k], outs[k], sems.at[k - 1]) for k in range(1, 7)]
     core = lax.axis_index("c")
     for k in (0, 1):
 
         @pl.when(core == k)
         def _():
-            low, high = LATE[k][0] * 128, (LATE[k][-1] + 1) * 128
-            done = [cols for cols in (slice(0, low), slice(high, 1152)) if cols.start < cols.stop]
+            late = LATE[k]
+            starts = [0] + [(tile + 1) * 128 for tile in late]
+            ends = [tile * 128 for tile in late] + [1152]
+            done = [slice(a, b) for a, b in zip(starts, ends) if a < b]
             copies = [
-                pltpu.make_async_copy(proj.at[:, cols], outs[0].at[:, cols], sems.at[7 * i])
+                pltpu.make_async_copy(proj.at[:, cols], outs[0].at[:, cols], sems.at[6 + i])
                 for i, cols in enumerate(done)
             ] + small
             for copy in copies:
                 copy.start()
-            whole = jnp.concatenate([w[tile] for tile in LATE[k]], axis=1)
+            whole = jnp.concatenate([w[tile] for tile in late], axis=1)
             for h in range(2):
                 some = slice(h * 256, h * 256 + 256)
-                buffer[some, 0 : high - low] = jnp.dot(
-                    nxt[some, :], whole, preferred_element_type=F32
-                ).astype(BF16)
-            last = pltpu.make_async_copy(
-                buffer.at[:, 0 : high - low], outs[0].at[:, low:high], late_sem
-            )
-            last.start()
-            for copy in copies + [last]:
+                buffer[some, :] = jnp.dot(nxt[some, :], whole, preferred_element_type=F32).astype(BF16)
+            for i, tile in enumerate(late):
+                last = pltpu.make_async_copy(
+                    buffer.at[:, i * 128 : i * 128 + 128],
+                    outs[0].at[:, tile * 128 : tile * 128 + 128],
+                    sems.at[9 + i],
+                )
+                last.start()
+                copies.append(last)
+            for copy in copies:
                 copy.wait()
 
 
@@ -641,7 +647,7 @@
         out_shape=results,
         in_specs=[vmem] * 9,
         out_specs=[large] * 7,
-        scratch_shapes=[DMA((8,)), DMA(()), pltpu.VMEM((512, 256), BF16)],
+        scratch_shapes=[DMA((11,)), pltpu.VMEM((512, 256), BF16)],
         compiler_params=pltpu.CompilerParams(vmem_limit_bytes=8 * 2**20),
         name="write_out",
     )(*inside)

time: 46.6 us -> 46.3 us (level)
  no operation moved by 1% of the time
where the time goes in v10:
time: 46.3 us; the launch traced here: 46.2 us
  Pallas kernels  45.4 us (98%)
  between operations  0.81 us (2%)
    pallas_call x1, Pallas kernels, shards(): pl.pallas_call(kernel, out_shape=[pltpu.VMEM(r.shape, r.dtype) for r in r...  44 us
    pallas_call x1, Pallas kernels, shards(): pl.pallas_call(write_out, out_shape=results, in_specs=[vmem] * 9, out_spe...  1.39 us

profile of v10, /device:TPU:1, one launch (start us, length us, event | category | flops | bytes accessed | tf_op | source)
XLA Modules:
  0.0 46.2 jit_solution(9855633865504102281)
XLA Ops:
  0.6 44.0 %step.1 = (bf16[512,1152]{1,0:T(8,128)(2,1)S(1)}, bf16[2,1152]{1,0:T(2,128)(2,1)S(1)}, f32[81,128]{1,0:T(8,128)S(1)}, f32[18,128]{1,0:T(8,128)S(1)}, f32[81,128]...) custom-call(bf16[512,1152]{1,0:T(8,128)(2,1)} %refs_0_.1, ...), custom_call_target="tpu_custom_call" | custom-call | tf_op jit(solution)/shard_map/step/pallas_call | solution.py:634
  44.6 1.4 %write_out.1 = (bf16[512,1152]{1,0:T(8,128)(2,1)}, bf16[2,1152]{1,0:T(2,128)(2,1)}, f32[81,128]{1,0:T(8,128)}, f32[18,128]{1,0:T(8,128)}, f32[81,128]{1,0:T(8,12...) custom-call(bf16[512,1152]{1,0:T(8,128)(2,1)S(1)} %get-tuple-element.23.refs_0_, bf16[2,1152]{1,0:T(2,128)(2,1)S(1)} %get-tuple-element.24.refs_1_, ...), custom_call_target="tpu_custom_call" | custom-call | tf_op jit(solution)/shard_map/write_out/pallas_call | solution.py:645
